TPU v7x, 128 devices: a whole 4x4x4 slice. The times are simulated.
128 devices in a mesh: ty: 8 (over y_hi, x), tx: 16 (over y_lo, z, core).
Axes of the slice: x: 4, y: 4 (y_hi: 2, y_lo: 2; y = y_hi * 2 + y_lo), z: 4, core: 2. Of those that a mesh axis runs over, the one named last changes fastest.
Arguments:
- surface_levels: float32 [1024, 32768], P('ty', 'tx'), may hold values from -6 to 6
- bearing_index: int32 [4], replicated, may hold values from 0 to 15
- stencil_displacements: int32 [4], replicated, may hold values from -4 to 4
- camera_altitude_class: int32 [4], replicated, may hold values from 0 to 3
Outputs:
- margin: float32 [4, 1024, 32768], P(None, 'ty', 'tx')
Inputs may be any that keep to these rules, and one draw needn't show every extreme that they name: `bearing_index`: azimuth indices.
All inputs are finite; a program needn't handle non-finite values.
Results may differ from a plain program's by a relative error of at most 0.00002.
Values sent between devices are 32-bit elements; how exact they have to be, the bound alone decides.
A program may use at most 192 MiB of HBM per device.

v0:
```python
import math

import jax
import jax.numpy as jnp
from jax import lax
from jax.sharding import PartitionSpec as P

AZIMUTHS = 4
STENCIL_REACH = 4


def padded(cells, sides, width):
    for axis, dim in sides:
        count = lax.axis_size(axis)
        ends = count - 1
        head = lax.slice_in_dim(cells, 0, width, axis=dim)
        tail = lax.slice_in_dim(cells, cells.shape[dim] - width, cells.shape[dim], axis=dim)
        cells = jnp.concatenate(
            [
                lax.ppermute(tail, axis, [(i, (i + 1) % count) for i in range(ends)]),
                cells,
                lax.ppermute(head, axis, [((i + 1) % count, i) for i in range(ends)]),
            ],
            axis=dim,
        )
    return cells


def copy_for_each(x, axis):
    devices = lax.axis_size(axis)
    return lax.all_to_all(jnp.broadcast_to(x[None], (devices, *x.shape)), axis, 0, 0, tiled=True)


def combined_pairwise(pieces, combine):
    while len(jax.tree.leaves(pieces)[0]) > 1:
        pieces = jax.vmap(combine)(*(pieces[side::2] for side in (0, 1)))
    return pieces[0]


def prefix(x, axis, combine, identity):
    devices, position = (lax.axis_size(axis), lax.axis_index(axis))
    passed = jnp.arange(devices) < position

    def kept(part, zero, own):
        part = jnp.where(
            passed.reshape(-1, *(1 for _ in own.shape)), part, jnp.asarray(zero, own.dtype)
        )
        return part

    pieces = copy_for_each(x, axis)
    return combined_pairwise(kept(pieces, identity, x), combine)


def view_tables(bearing_index, camera_altitude_class, easting_span):
    angle_idx = bearing_index.astype(jnp.float32)
    frac = ((bearing_index * 5 % 16).astype(jnp.float32) + 0.5) / 16.0
    theta = (angle_idx - 7.5) * (math.pi / 32.0)
    stride = 1.0 / jnp.cos(theta)
    slope = (1.0 + camera_altitude_class.astype(jnp.float32)) / (4.0 * easting_span)
    cube = frac * frac * frac
    square = frac * frac
    weights = jnp.stack(
        [
            (-cube + 2.0 * square - frac) / 2.0,
            (3.0 * cube - 5.0 * square + 2.0) / 2.0,
            (-3.0 * cube + 4.0 * square + frac) / 2.0,
            (cube - square) / 2.0,
        ],
        axis=1,
    )
    return (weights, stride * slope)


def on_device(surface_levels, bearing_index, stencil_displacements, camera_altitude_class):
    northing_extent, easting_extent = surface_levels.shape
    easting_span = easting_extent * lax.axis_size("tx")
    weights, rise = view_tables(bearing_index, camera_altitude_class, easting_span)
    bordered_surface = padded(surface_levels, (("ty", 0),), STENCIL_REACH + 2)
    first_col = lax.axis_index("tx") * easting_extent
    columns = (first_col + jnp.arange(easting_extent)).astype(jnp.float32)
    stacked = []
    for which in range(AZIMUTHS):
        strips = jnp.zeros((northing_extent, easting_extent), jnp.float32)
        for tap_index in range(4):
            start = stencil_displacements[which] + tap_index + STENCIL_REACH + 1
            strips = strips + weights[which, tap_index] * lax.dynamic_slice_in_dim(
                bordered_surface, start, northing_extent, 0
            )
        stacked.append(strips + rise[which] * columns[None, :])
    lifted = jnp.stack(stacked, axis=0)
    running = lax.cummax(lifted, axis=2)
    row_peak = running[:, :, -1]
    before = prefix(row_peak, "tx", jnp.maximum, jnp.full_like(row_peak, -jnp.inf))
    lowest = jnp.full((AZIMUTHS, northing_extent, 1), -jnp.inf, jnp.float32)
    earlier = jnp.concatenate([lowest, running[:, :, :-1]], axis=2)
    horizon = jnp.maximum(earlier, before[:, :, None])
    margin = jnp.maximum(horizon - lifted, 0.0)
    return margin


def solution(mesh):
    return jax.shard_map(
        on_device,
        mesh=mesh,
        in_specs=(P("ty", "tx"), P(), P(), P()),
        out_specs=P(None, "ty", "tx"),
        check_vma=False,
    )
```

profile of v0, /device:TPU:17, one launch (start us, length us, event | category | flops | bytes accessed | tf_op | source)
XLA Modules:
  0.0 91.1 jit_solution(12587648940811494486)
XLA Ops:
  0.0 0.9 fusion.16
  0.9 3.1 %collective-permute-start = (f32[6,2048]{1,0:T(8,128)S(1)}, f32[6,2048]{1,0:T(8,128)S(1)}, u32[]{:S(2)}, u32[]{:S(2)}) collective-permute-start(f32[6,2048]{1,0:T(8,128)S(1)} %get-tuple-element.11), channel_id=1, source_target_pairs={{0,16},{16,32},{32,48},{48,64},{64,80},{80,96},{96,112},{1,17},{17... | collective-permute-start | bytes 147464 | tf_op jit(solution)/shard_map/ppermute | solution.py:20
  4.0 5.8 %collective-permute-start.1 = (f32[6,2048]{1,0:T(8,128)S(1)}, f32[6,2048]{1,0:T(8,128)S(1)}, u32[]{:S(2)}, u32[]{:S(2)}) collective-permute-start(f32[6,2048]{1,0:T(8,128)S(1)} %get-tuple-element.12), channel_id=1, source_target_pairs={{16,0},{32,16},{48,32},{64,48},{80,64},{96,80},{112,96},{17,1},{33... | collective-permute-start | bytes 147464 | tf_op jit(solution)/shard_map/ppermute | solution.py:22
  9.8 0.8 subtract_multiply_fusion.1
  10.6 0.7 fusion.20
  11.3 1.5 %fusion.22 = (s32[1]{0:T(128)}, s32[1]{0:T(128)}, s32[1]{0:T(128)}, s32[1]{0:T(128)}) fusion(s32[4]{0:T(128)} %param.6), kind=kLoop, calls=%fused_computation.49 | loop fusion | bytes 32 | tf_op jit(solution)/shard_map/slice | solution.py:85
  12.7 0.7 fusion.17
  13.4 0.7 convert_multiply_fusion.2
  14.1 0.7 convert_multiply_fusion.1
  14.8 0.7 convert_multiply_fusion
  15.5 0.7 fusion.18
  37.1 1.6 %copy.19 = f32[128,2048]{0,1:T(8,128)S(1)} copy(f32[128,2048]{1,0:T(8,128)} %param.4) | data formatting | bytes 2097152 | tf_op args[0]
  39.6 0.9 pad_maximum_fusion
  40.5 7.9 %add_add_fusion.2 = (f32[128,2048]{0,1:T(8,128)S(1)}, f32[128,2048]{0,1:T(8,128)S(1)}) fusion(f32[140,2048]{0,1:T(8,128)S(1)} %pad_maximum_fusion, s32[]{:T(128)S(6)} %select_n.67, s32[]{:T(128)S(6)} %select_n.66, s32[]{:T(128)S(6)} %select_n.65, s32[]{:T(128)S(6)} %select_n.64, f32[2048]{0:T(1024)S(1)} %convert_multiply_fusion.2, f32[]{:T(128)} %bitcast.23, ...), kind=kLoop, calls=%fused_computation.14 | loop fusion | flops 4194304 | bytes 10502208 | tf_op jit(solution)/shard_map/add | solution.py:89
  49.6 8.0 %add_add_fusion.3 = (f32[128,2048]{0,1:T(8,128)S(1)}, f32[128,2048]{0,1:T(8,128)S(1)}) fusion(f32[140,2048]{0,1:T(8,128)S(1)} %pad_maximum_fusion, s32[]{:T(128)S(6)} %select_n.63, s32[]{:T(128)S(6)} %select_n.62, s32[]{:T(128)S(6)} %select_n.61, s32[]{:T(128)S(6)} %select_n.60, f32[2048]{0:T(1024)S(1)} %convert_multiply_fusion.3, f32[]{:T(128)} %bitcast.9, ...), kind=kLoop, calls=%fused_computation.15 | loop fusion | flops 4194304 | bytes 10502208 | tf_op jit(solution)/shard_map/add | solution.py:89
  59.5 2.0 %copy-done = f32[4,128,16,128]{1,2,3,0:T(8,128)} copy-done((f32[4,128,16,128]{1,2,3,0:T(8,128)}, f32[4,128,16,128]{1,2,3,0:T(8,128)S(1)}, u32[]{:S(2)}) %copy-start) | copy-done | bytes 4194328
  61.6 2.6 %broadcast_maximum_fusion = f32[4,128,16,128]{1,2,3,0:T(8,128)S(1)} fusion(f32[4,128,16,128]{1,2,3,0:T(8,128)} %copy-done, f32[4,128,16]{1,2,0:T(8,128)S(1)} %slice.183), kind=kLoop, calls=%fused_computation.11 | loop fusion | flops 1048576 | bytes 8421376 | tf_op jit(solution)/shard_map/reduce_window_max | solution.py:91
  64.2 1.3 %copy.25 = f32[4,128,16,128]{1,3,2,0:T(8,128)S(1)} copy(f32[4,128,16,128]{1,2,3,0:T(8,128)S(1)} %broadcast_maximum_fusion) | data formatting | bytes 8388608 | tf_op jit(solution)/shard_map/reduce_window_max | solution.py:91
  65.5 2.0 %copy-done.1 = f32[4,128,16,128]{1,3,2,0:T(8,128)} copy-done((f32[4,128,16,128]{1,3,2,0:T(8,128)}, f32[4,128,16,128]{1,3,2,0:T(8,128)S(1)}, u32[]{:S(2)}) %copy-start.1) | copy-done | bytes 4194328
  67.5 0.6 broadcast_in_dim.27
  68.2 7.3 %all-to-all-start = ((f32[16,4,128]{2,1,0:T(4,128)}), f32[16,4,128]{2,1,0:T(4,128)S(1)}, u32[]{:S(2)}, u32[]{:S(2)}) async-start(f32[16,4,128]{2,1,0:T(4,128)} %broadcast_in_dim.27), calls=%async_computation | async-start | bytes 65536 | tf_op jit(solution)/shard_map/all_to_all | solution.py:31
  75.4 5.8 %all-to-all-done = f32[16,4,128]{2,1,0:T(4,128)S(1)} async-done(((f32[16,4,128]{2,1,0:T(4,128)}), f32[16,4,128]{2,1,0:T(4,128)S(1)}, u32[]{:S(2)}, u32[]{:S(2)}) %all-to-all-start) | async-done | bytes 32800 | tf_op jit(solution)/shard_map/all_to_all | solution.py:31
  81.4 4.3 %fusion.8 = f32[4,128,2048]{1,2,0:T(8,128)} fusion(f32[1,128,2048]{1,2,0:T(8,128)S(1)} %bitcast.72, f32[1,128,2048]{1,2,0:T(8,128)} %bitcast.76, f32[1,128,2048]{1,2,0:T(8,128)S(1)} %bitcast.70, f32[1,128,2048]{1,2,0:T(8,128)S(1)} %bitcast.74, f32[4,128,2047]{1,2,0:T(8,128)} %bitcast.68, f32[4,128]{1,0:T(4,128)S(1)} %fusion.9), kind=kLoop, calls=%fused_computation.9 | loop fusion | flops 6291456 | bytes 12582912 | tf_op jit(solution)/shard_map/max | solution.py:97
  85.7 5.3 %copy.26 = f32[4,128,2048]{2,1,0:T(8,128)} copy(f32[4,128,2048]{1,2,0:T(8,128)} %fusion.8) | data formatting | bytes 8388608 | tf_op jit(solution)/shard_map/max | solution.py:97
  (25 shorter events, 4.6 us)
Async XLA Ops:
  0.9 38.3 %collective-permute-start = (f32[6,2048]{1,0:T(8,128)S(1)}, f32[6,2048]{1,0:T(8,128)S(1)}, u32[]{:S(2)}, u32[]{:S(2)}) collective-permute-start(f32[6,2048]{1,0:T(8,128)S(1)} %get-tuple-element.11), channel_id=1, source_target_pairs={{0,16},{16,32},{32,48},{48,64},{64,80},{80,96},{96,112},{1,17},{17... | collective-permute-start | bytes 147464 | tf_op jit(solution)/shard_map/ppermute | solution.py:20
  4.0 34.8 %collective-permute-start.1 = (f32[6,2048]{1,0:T(8,128)S(1)}, f32[6,2048]{1,0:T(8,128)S(1)}, u32[]{:S(2)}, u32[]{:S(2)}) collective-permute-start(f32[6,2048]{1,0:T(8,128)S(1)} %get-tuple-element.12), channel_id=1, source_target_pairs={{16,0},{32,16},{48,32},{64,48},{80,64},{96,80},{112,96},{17,1},{33... | collective-permute-start | bytes 147464 | tf_op jit(solution)/shard_map/ppermute | solution.py:22
  57.6 1.0 %copy-start.2 = (f32[128,2048]{0,1:T(8,128)}, f32[128,2048]{0,1:T(8,128)S(1)}, u32[]{:S(2)}) copy-start(f32[128,2048]{0,1:T(8,128)S(1)} %get-tuple-element.8) | copy-start | bytes 3145732
  59.5 2.0 %copy-start = (f32[4,128,16,128]{1,2,3,0:T(8,128)}, f32[4,128,16,128]{1,2,3,0:T(8,128)S(1)}, u32[]{:S(2)}) copy-start(f32[4,128,16,128]{1,2,3,0:T(8,128)S(1)} %fusion) | copy-start | bytes 12582916
  65.5 2.0 %copy-start.1 = (f32[4,128,16,128]{1,3,2,0:T(8,128)}, f32[4,128,16,128]{1,3,2,0:T(8,128)S(1)}, u32[]{:S(2)}) copy-start(f32[4,128,16,128]{1,3,2,0:T(8,128)S(1)} %copy.25) | copy-start | bytes 12582916
  68.2 13.1 %all-to-all-start = ((f32[16,4,128]{2,1,0:T(4,128)}), f32[16,4,128]{2,1,0:T(4,128)S(1)}, u32[]{:S(2)}, u32[]{:S(2)}) async-start(f32[16,4,128]{2,1,0:T(4,128)} %broadcast_in_dim.27), calls=%async_computation | async-start | bytes 65536 | tf_op jit(solution)/shard_map/all_to_all | solution.py:31
where the time goes:
time: 91.9 us; the launch traced here: 91.1 us
  other arithmetic  27.7 us (30%)
  local copies, waits for them, and re-layouts  20.7 us (23%)
  between operations  20.7 us (23%)
  starting transfers between devices  16.2 us (18%)
  waiting for transfers between devices  5.8 us (6%)
    add x2, other arithmetic, on_device(): stacked.append(strips + rise[which] * columns[None, :])  15.9 us
    all_to_all x1, starting transfers between devices, copy_for_each(): lax.all_to_all(jnp.broadcast_to(x[None], (devices, *x.shape)), axis, 0, 0...  7.28 us
    unnamed x7, local copies, waits for them, and re-layouts  5.9 us
    all_to_all x1, waiting for transfers between devices, copy_for_each(): lax.all_to_all(jnp.broadcast_to(x[None], (devices, *x.shape)), axis, 0, 0...  5.79 us
    ppermute x1, starting transfers between devices, padded(): lax.ppermute(head, axis, [((i + 1) % count, i) for i in range(ends)])  5.78 us
    max x1, local copies, waits for them, and re-layouts, on_device(): margin = jnp.maximum(horizon - lifted, 0.0)  5.34 us
    max x1, other arithmetic, on_device(): margin = jnp.maximum(horizon - lifted, 0.0)  4.35 us
    ppermute x1, starting transfers between devices, padded(): lax.ppermute(tail, axis, [(i, (i + 1) % count) for i in range(ends)])  3.12 us
  transfers between devices with their start and end apart: 3, of which 1 were waited for; matrix products, arithmetic and copies ran while one was open for 10% of the time, Pallas kernels for 0%

commit v1 on v0

v1 whole, which is shorter than its diff:
```python
import functools
import math

import jax
import jax.numpy as jnp
from jax import lax
from jax.experimental import pallas as pl
from jax.experimental.pallas import tpu as pltpu
from jax.sharding import PartitionSpec as P

VIEWS = 4
ROWS = 128
LANES = 128
NEG = -jnp.inf


def tables(bearing, camera, k, span):
    a = jnp.full((8, LANES), bearing[k], jnp.int32)
    cls = jnp.full((8, LANES), camera[k], jnp.int32).astype(jnp.float32)
    f = (((a * 5) & 15).astype(jnp.float32) + 0.5) / 16.0
    theta = (a.astype(jnp.float32) - 7.5) * (math.pi / 32.0)
    stride = 1.0 / jnp.cos(theta)
    slope = (1.0 + cls) / (4.0 * span)
    cube = f * f * f
    square = f * f
    taps = (
        (-cube + 2.0 * square - f) / 2.0,
        (3.0 * cube - 5.0 * square + 2.0) / 2.0,
        (-3.0 * cube + 4.0 * square + f) / 2.0,
        (cube - square) / 2.0,
    )
    return taps, stride * slope


def kernel(
    nty, ntx, chunks, early,
    x_hbm, bearing_hbm, shift_hbm, camera_hbm, out,
    bearing, shift, camera, xs, top, bot, ls, wv, peaks, bpeaks, msg_i, msg_b, in_i, in_b, bsplat_i, bsplat_b,
    in_sem, tab_sem, halo_send, halo_recv, pre_send_i, pre_recv_i, pre_send_b, pre_recv_b,
):
    ty = lax.axis_index("ty")
    tx = lax.axis_index("tx")
    width = chunks * LANES
    span = width * ntx
    has_up = ty > 0
    has_down = ty < nty - 1

    in_i[...] = jnp.full(in_i.shape, NEG, jnp.float32)
    in_b[...] = jnp.full(in_b.shape, NEG, jnp.float32)

    loads = [
        pltpu.make_async_copy(
            x_hbm.at[:, pl.ds(c * LANES, LANES)], xs.at[c], in_sem.at[c]
        )
        for c in range(chunks)
    ]
    small = [
        pltpu.make_async_copy(src, dst, tab_sem.at[n])
        for n, (src, dst) in enumerate(
            ((bearing_hbm, bearing), (shift_hbm, shift), (camera_hbm, camera))
        )
    ]
    for copy in small + loads:
        copy.start()

    barrier = pltpu.get_barrier_semaphore()

    def greet(p):
        pl.semaphore_signal(barrier, inc=1, device_id=p, device_id_type=pl.DeviceIdType.MESH)

    @pl.when(has_up)
    def _():
        greet({"ty": ty - 1, "tx": tx})

    @pl.when(has_down)
    def _():
        greet({"ty": ty + 1, "tx": tx})

    for p in range(ntx):
        @pl.when(p < tx)
        def _():
            greet({"ty": ty, "tx": p})

    for copy in small:
        copy.wait()

    for k in range(VIEWS):
        taps, rise = tables(bearing, camera, k, span)
        for j in range(4):
            wv[k, j] = taps[j]
        wv[k, 4] = rise

    for copy in loads:
        copy.wait()
    for c in range(chunks):
        top[c, 8:24] = xs[c, 0:16]
        bot[c, 0:16] = xs[c, ROWS - 16:ROWS]

    @pl.when(jnp.logical_not(has_up))
    def _():
        for c in range(chunks):
            top[c, 0:8] = jnp.zeros((8, LANES), jnp.float32)

    @pl.when(jnp.logical_not(has_down))
    def _():
        for c in range(chunks):
            bot[c, 16:24] = jnp.zeros((8, LANES), jnp.float32)

    lane = lax.broadcasted_iota(jnp.int32, (8, LANES), 1)
    first = tx * width

    def tile_scan(src, base, row, want_peak):
        result = []
        for k in range(VIEWS):
            w = [wv[k, j] for j in range(4)]
            rise = wv[k, 4]
            start = base + shift[k]
            carry = None
            for c in range(chunks):
                acc = w[0] * src[c, pl.ds(start - 1, 8), :]
                for j in range(1, 4):
                    acc = acc + w[j] * src[c, pl.ds(start + j - 1, 8), :]
                cols = (lane + (first + c * LANES)).astype(jnp.float32)
                lifted = acc + rise * cols
                ls[k, pl.ds(row, 8), pl.ds(c * LANES, LANES)] = lifted
                run = lifted
                step = 1
                while step < LANES:
                    run = jnp.maximum(run, jnp.where(lane >= step, pltpu.roll(run, step, 1), NEG))
                    step *= 2
                if carry is not None:
                    run = jnp.maximum(run, carry)
                out[k, pl.ds(row, 8), pl.ds(c * LANES, LANES)] = run
                carry = jnp.broadcast_to(run[:, LANES - 1:LANES], (8, LANES))
            result.append(carry)
        return result

    def interior(i, _):
        row = pl.multiple_of(i * 8, 8)
        for k, peak in enumerate(tile_scan(xs, row, row, True)):
            peaks[k, pl.ds(row, 8), :] = peak
        return 0

    for k in range(VIEWS):
        peaks[k, 0:8, :] = jnp.full((8, LANES), NEG, jnp.float32)
        peaks[k, ROWS - 8:ROWS, :] = jnp.full((8, LANES), NEG, jnp.float32)

    tiles = ROWS // 8
    lax.fori_loop(1, 1 + early, interior, 0)

    waits = (ntx - 1 - tx) + has_up.astype(jnp.int32) + has_down.astype(jnp.int32)
    pl.semaphore_wait(barrier, waits)

    up = pltpu.make_async_remote_copy(
        src_ref=xs.at[:, pl.ds(0, 8), :], dst_ref=bot.at[:, pl.ds(16, 8), :],
        send_sem=halo_send.at[0], recv_sem=halo_recv.at[0],
        device_id={"ty": ty - 1, "tx": tx}, device_id_type=pl.DeviceIdType.MESH,
    )
    down = pltpu.make_async_remote_copy(
        src_ref=xs.at[:, pl.ds(ROWS - 8, 8), :], dst_ref=top.at[:, pl.ds(0, 8), :],
        send_sem=halo_send.at[1], recv_sem=halo_recv.at[1],
        device_id={"ty": ty + 1, "tx": tx}, device_id_type=pl.DeviceIdType.MESH,
    )

    @pl.when(has_up)
    def _():
        up.start()

    @pl.when(has_down)
    def _():
        down.start()

    lax.fori_loop(1 + early, tiles - 1, interior, 0)

    def spread(msg, store, send, recv):
        copies = {
            p: pltpu.make_async_remote_copy(
                src_ref=msg, dst_ref=store.at[tx], send_sem=send.at[p], recv_sem=recv.at[tx],
                device_id={"ty": ty, "tx": p}, device_id_type=pl.DeviceIdType.MESH,
            )
            for p in range(1, ntx)
        }
        for p in range(1, ntx):
            @pl.when(p > tx)
            def _():
                copies[p].start()
        return copies

    def finish_sends(copies):
        for p in range(1, ntx):
            @pl.when(p > tx)
            def _():
                copies[p].wait_send()

    def receive(msg, store, recv):
        for p in range(ntx - 1):
            @pl.when(p < tx)
            def _():
                pltpu.make_async_remote_copy(
                    src_ref=msg, dst_ref=store.at[p], send_sem=recv.at[p], recv_sem=recv.at[p],
                    device_id={"ty": ty, "tx": p}, device_id_type=pl.DeviceIdType.MESH,
                ).wait_recv()

    for k in range(VIEWS):
        msg_i[k] = jnp.max(peaks[k].T, axis=0, keepdims=True)
    sent_i = spread(msg_i, in_i, pre_send_i, pre_recv_i)

    @pl.when(has_down)
    def _():
        up_in = pltpu.make_async_remote_copy(
            src_ref=xs.at[:, pl.ds(0, 8), :], dst_ref=bot.at[:, pl.ds(16, 8), :],
            send_sem=halo_send.at[0], recv_sem=halo_recv.at[0],
            device_id={"ty": ty + 1, "tx": tx}, device_id_type=pl.DeviceIdType.MESH,
        )
        up_in.wait_recv()

    @pl.when(has_up)
    def _():
        down_in = pltpu.make_async_remote_copy(
            src_ref=xs.at[:, pl.ds(ROWS - 8, 8), :], dst_ref=top.at[:, pl.ds(0, 8), :],
            send_sem=halo_send.at[1], recv_sem=halo_recv.at[1],
            device_id={"ty": ty - 1, "tx": tx}, device_id_type=pl.DeviceIdType.MESH,
        )
        down_in.wait_recv()

    bpeaks[...] = jnp.full(bpeaks.shape, NEG, jnp.float32)
    for k, peak in enumerate(tile_scan(top, 8, 0, True)):
        bpeaks[16 * k:16 * k + 8, :] = peak
    for k, peak in enumerate(tile_scan(bot, 8, ROWS - 8, True)):
        bpeaks[16 * k + 8:16 * k + 16, :] = peak
    msg_b[...] = jnp.max(bpeaks[...].T, axis=0, keepdims=True)
    sent_b = spread(msg_b, in_b, pre_send_b, pre_recv_b)

    receive(msg_i, in_i, pre_recv_i)
    for k in range(VIEWS):
        best = in_i[0, k]
        for p in range(1, ntx):
            best = jnp.maximum(best, in_i[p, k])
        bsplat_i[k] = jnp.broadcast_to(best, (LANES, LANES)).T

    def close(k, row, before):
        for c in range(chunks):
            at = (k, pl.ds(row, 8), pl.ds(c * LANES, LANES))
            out[at] = jnp.maximum(out[at], before) - ls[at]

    def close_interior(i, _):
        row = pl.multiple_of(i * 8, 8)
        for k in range(VIEWS):
            close(k, row, bsplat_i[k, pl.ds(row, 8), :])
        return 0

    lax.fori_loop(1, tiles - 1, close_interior, 0)

    receive(msg_b, in_b, pre_recv_b)
    best = in_b[0]
    for p in range(1, ntx):
        best = jnp.maximum(best, in_b[p])
    bsplat_b[...] = jnp.broadcast_to(best, (LANES, LANES)).T
    for k in range(VIEWS):
        close(k, 0, bsplat_b[16 * k:16 * k + 8, :])
        close(k, ROWS - 8, bsplat_b[16 * k + 8:16 * k + 16, :])

    @pl.when(has_up)
    def _():
        up.wait_send()

    @pl.when(has_down)
    def _():
        down.wait_send()

    finish_sends(sent_i)
    finish_sends(sent_b)


def on_device(surface_levels, bearing_index, stencil_displacements, camera_altitude_class):
    rows, width = surface_levels.shape
    nty, ntx = lax.axis_size("ty"), lax.axis_size("tx")
    chunks = width // LANES
    vm = lambda *s: pltpu.VMEM(s, jnp.float32)
    return pl.pallas_call(
        functools.partial(kernel, nty, ntx, chunks, 4),
        out_shape=jax.ShapeDtypeStruct((VIEWS, rows, width), jnp.float32),
        in_specs=[pl.BlockSpec(memory_space=pltpu.HBM)] * 4,
        out_specs=pl.BlockSpec(memory_space=pltpu.VMEM),
        scratch_shapes=[
            pltpu.SMEM((VIEWS,), jnp.int32), pltpu.SMEM((VIEWS,), jnp.int32),
            pltpu.SMEM((VIEWS,), jnp.int32),
            vm(chunks, ROWS, LANES), vm(chunks, 24, LANES), vm(chunks, 24, LANES),
            vm(VIEWS, rows, width), vm(VIEWS, 5, 8, LANES),
            vm(VIEWS, ROWS, LANES), vm(LANES, LANES),
            vm(VIEWS, 1, LANES), vm(1, LANES),
            vm(ntx, VIEWS, 1, LANES), vm(ntx, 1, LANES),
            vm(VIEWS, LANES, LANES), vm(LANES, LANES),
            pltpu.SemaphoreType.DMA((chunks,)),
            pltpu.SemaphoreType.DMA((3,)),
            pltpu.SemaphoreType.DMA((2,)), pltpu.SemaphoreType.DMA((2,)),
            pltpu.SemaphoreType.DMA((ntx,)), pltpu.SemaphoreType.DMA((ntx,)),
            pltpu.SemaphoreType.DMA((ntx,)), pltpu.SemaphoreType.DMA((ntx,)),
        ],
        compiler_params=pltpu.CompilerParams(
            collective_id=0, has_side_effects=True, vmem_limit_bytes=40 * 1024 * 1024
        ),
        name="horizon",
    )(surface_levels, bearing_index, stencil_displacements, camera_altitude_class)


def solution(mesh):
    return jax.shard_map(
        on_device,
        mesh=mesh,
        in_specs=(P("ty", "tx"), P(), P(), P()),
        out_specs=P(None, "ty", "tx"),
        check_vma=False,
    )
```

time: 91.9 us -> 38.4 us (0.42)
  the two profiles are of different devices: /device:TPU:17 before, /device:TPU:24 now
where the time goes in v1:
time: 38.4 us; the launch traced here: 38.2 us
  Pallas kernels  33 us (86%)
  local copies, waits for them, and re-layouts  5.2 us (14%)
    pallas_call x1, Pallas kernels, on_device(): pl.pallas_call(functools.partial(kernel, nty, ntx, chunks, 4), out_shape=...  33 us
    unnamed x9, local copies, waits for them, and re-layouts  5.2 us

profile of v1, /device:TPU:24, one launch (start us, length us, event | category | flops | bytes accessed | tf_op | source)
XLA Modules:
  0.0 38.2 jit_solution(18059320920981114740)
XLA Ops:
  0.0 0.0 copy-start
  0.0 1.2 %copy-done = f32[128,2048]{1,0:T(8,128)S(1)} copy-done((f32[128,2048]{1,0:T(8,128)S(1)}, f32[128,2048]{1,0:T(8,128)}, u32[]{:S(2)}) %copy-start) | copy-done | bytes 1048600
  1.2 0.0 copy-start.1
  1.2 0.7 %copy-done.1 = s32[4]{0:T(128)S(1)} copy-done((s32[4]{0:T(128)S(1)}, s32[4]{0:T(128)}, u32[]{:S(2)}) %copy-start.1) | copy-done | bytes 40
  1.9 0.0 copy-start.2
  1.9 0.7 %copy-done.2 = s32[4]{0:T(128)S(1)} copy-done((s32[4]{0:T(128)S(1)}, s32[4]{0:T(128)}, u32[]{:S(2)}) %copy-start.2) | copy-done | bytes 40
  2.5 0.0 copy-start.3
  2.5 0.7 %copy-done.3 = s32[4]{0:T(128)S(1)} copy-done((s32[4]{0:T(128)S(1)}, s32[4]{0:T(128)}, u32[]{:S(2)}) %copy-start.3) | copy-done | bytes 40
  3.2 33.0 %horizon.1 = f32[4,128,2048]{2,1,0:T(8,128)S(1)} custom-call(f32[128,2048]{1,0:T(8,128)S(1)} %copy-done, s32[4]{0:T(128)S(1)} %copy-done.1, s32[4]{0:T(128)S(1)} %copy-done.2, s32[4]{0:T(128)S(1)} %copy-done.3), custom_call_target="tpu_custom_call" | custom-call | tf_op jit(solution)/shard_map/horizon/pallas_call | solution.py:280
  36.2 2.0 %copy.6 = f32[4,128,2048]{2,1,0:T(8,128)} copy(f32[4,128,2048]{2,1,0:T(8,128)S(1)} %horizon.1) | data formatting | bytes 8388608
Async XLA Ops:
  0.0 1.2 %copy-start = (f32[128,2048]{1,0:T(8,128)S(1)}, f32[128,2048]{1,0:T(8,128)}, u32[]{:S(2)}) copy-start(f32[128,2048]{1,0:T(8,128)} %x_hbm.1) | copy-start | bytes 3145732
  1.2 0.7 %copy-start.1 = (s32[4]{0:T(128)S(1)}, s32[4]{0:T(128)}, u32[]{:S(2)}) copy-start(s32[4]{0:T(128)} %bearing_hbm.1) | copy-start | bytes 52
  1.9 0.7 %copy-start.2 = (s32[4]{0:T(128)S(1)}, s32[4]{0:T(128)}, u32[]{:S(2)}) copy-start(s32[4]{0:T(128)} %shift_hbm.1) | copy-start | bytes 52
  2.5 0.7 %copy-start.3 = (s32[4]{0:T(128)S(1)}, s32[4]{0:T(128)}, u32[]{:S(2)}) copy-start(s32[4]{0:T(128)} %camera_hbm.1) | copy-start | bytes 52

commit v2 on v1

v2 whole, which is shorter than its diff:
```python
import functools
import math

import jax
import jax.numpy as jnp
from jax import lax
from jax.experimental import pallas as pl
from jax.experimental.pallas import tpu as pltpu
from jax.sharding import PartitionSpec as P

VIEWS = 4
ROWS = 128
LANES = 128
NEG = -jnp.inf


def tables(bearing, camera, k, span):
    a = jnp.full((8, LANES), bearing[k], jnp.int32)
    cls = jnp.full((8, LANES), camera[k], jnp.int32).astype(jnp.float32)
    f = (((a * 5) & 15).astype(jnp.float32) + 0.5) / 16.0
    theta = (a.astype(jnp.float32) - 7.5) * (math.pi / 32.0)
    stride = 1.0 / jnp.cos(theta)
    slope = (1.0 + cls) / (4.0 * span)
    cube = f * f * f
    square = f * f
    taps = (
        (-cube + 2.0 * square - f) / 2.0,
        (3.0 * cube - 5.0 * square + 2.0) / 2.0,
        (-3.0 * cube + 4.0 * square + f) / 2.0,
        (cube - square) / 2.0,
    )
    return taps, stride * slope


def sub_scan(total, sub):
    for step in (1, 2, 4):
        total = jnp.maximum(total, jnp.where(sub >= step, pltpu.roll(total, step, 0), NEG))
    return total


def kernel(
    nty, ntx, chunks, group, early,
    x_hbm, bearing_hbm, shift_hbm, camera_hbm, out,
    bearing, shift, camera, xs, top, bot, ls, wv, flat, scan,
    bpeaks, msg_i, msg_b, in_i, in_b, bsplat_i, bsplat_b, held,
    in_sem, tab_sem, ready, halo_send, halo_recv,
    pre_send_i, pre_recv_i, pre_send_b, pre_recv_b,
):
    ty = lax.axis_index("ty")
    tx = lax.axis_index("tx")
    width = chunks * LANES
    span = width * ntx
    tiles = ROWS // 8
    has_up = ty > 0
    has_down = ty < nty - 1
    mesh_id = pl.DeviceIdType.MESH

    in_i[...] = jnp.full(in_i.shape, NEG, jnp.float32)
    in_b[...] = jnp.full(in_b.shape, NEG, jnp.float32)

    barrier = pltpu.get_barrier_semaphore()

    def greet(p):
        pl.semaphore_signal(barrier, inc=1, device_id=p, device_id_type=mesh_id)

    @pl.when(has_up)
    def _():
        greet({"ty": ty - 1, "tx": tx})

    @pl.when(has_down)
    def _():
        greet({"ty": ty + 1, "tx": tx})

    for p in range(1, ntx):
        @pl.when(p > tx)
        def _():
            greet({"ty": ty, "tx": p})

    loads = [
        pltpu.make_async_copy(
            x_hbm.at[:, pl.ds(c * LANES, LANES)], xs.at[c], in_sem.at[c]
        )
        for c in range(chunks)
    ]
    small = [
        pltpu.make_async_copy(src, dst, tab_sem.at[n])
        for n, (src, dst) in enumerate(
            ((bearing_hbm, bearing), (shift_hbm, shift), (camera_hbm, camera))
        )
    ]
    for copy in small + loads:
        copy.start()
    for copy in small:
        copy.wait()

    for k in range(VIEWS):
        taps, rise = tables(bearing, camera, k, span)
        for j in range(4):
            wv[k, j] = taps[j]
        wv[k, 4] = rise

    for copy in loads:
        copy.wait()

    lane = lax.broadcasted_iota(jnp.int32, (8, LANES), 1)
    sub = lax.broadcasted_iota(jnp.int32, (8, LANES), 0)
    first = tx * width

    def ramp(k, c):
        return wv[k, 4] * (lane + (first + c * LANES)).astype(jnp.float32)

    def lift(src, c, k, start, slant):
        acc = wv[k, 0] * src[c, pl.ds(start - 1, 8), :]
        for j in range(1, 4):
            acc = acc + wv[k, j] * src[c, pl.ds(start + j - 1, 8), :]
        return acc + slant

    blank = jnp.zeros((8, LANES), jnp.float32)

    def block(c, k, n, carry):
        cols = pl.ds(pl.multiple_of(c * LANES, LANES), LANES)
        slant = ramp(k, c)
        parts = [blank]
        for i in range(1, tiles - 1):
            part = lift(xs, c, k, 8 * i + shift[k], slant)
            ls[k, 8 * i:8 * i + 8, cols] = part
            parts.append(part)
        parts.append(blank)
        turned = jnp.concatenate(parts, axis=0).T
        for t in range(16):
            at = 8 * t + t // 2
            flat[n, at:at + 8, :] = turned[8 * t:8 * t + 8]
        runs = [flat[n, pl.ds(0, 8, stride=17), :]]
        for u in range(1, 16):
            runs.append(jnp.maximum(runs[-1], flat[n, pl.ds(u, 8, stride=17), :]))
        total = sub_scan(runs[-1], sub)
        before = jnp.maximum(jnp.where(sub >= 1, pltpu.roll(total, 1, 0), NEG), carry)
        carry = jnp.maximum(carry, jnp.broadcast_to(total[7:8], (8, LANES)))
        for u in range(16):
            scan[n, pl.ds(u, 8, stride=17), :] = jnp.maximum(runs[u], before)
        whole = jnp.concatenate(
            [scan[n, 8 * t + t // 2:8 * t + t // 2 + 8, :] for t in range(16)], axis=0
        ).T
        for i in range(1, tiles - 1):
            out[k, 8 * i:8 * i + 8, cols] = whole[8 * i:8 * i + 8]
        return carry

    def interior(g, carries):
        carries = list(carries)
        for q in range(group):
            for k in range(VIEWS):
                carries[k] = block(g * group + q, k, q * VIEWS + k, carries[k])
        return tuple(carries)

    carries = tuple(jnp.full((8, LANES), NEG, jnp.float32) for _ in range(VIEWS))
    carries = lax.fori_loop(0, early, interior, carries)

    for c in range(chunks):
        top[c, 8:24] = xs[c, 0:16]
        bot[c, 0:16] = xs[c, ROWS - 16:ROWS]

    @pl.when(jnp.logical_not(has_up))
    def _():
        for c in range(chunks):
            top[c, 0:8] = blank

    @pl.when(jnp.logical_not(has_down))
    def _():
        for c in range(chunks):
            bot[c, 16:24] = blank

    pl.semaphore_wait(barrier, tx + has_up.astype(jnp.int32) + has_down.astype(jnp.int32))

    def halo(n, src_row, dst, dst_row, peer):
        return pltpu.make_async_remote_copy(
            src_ref=xs.at[:, pl.ds(src_row, 8), :], dst_ref=dst.at[:, pl.ds(dst_row, 8), :],
            send_sem=halo_send.at[n], recv_sem=halo_recv.at[n],
            device_id={"ty": peer, "tx": tx}, device_id_type=mesh_id,
        )

    @pl.when(has_up)
    def _():
        halo(0, 0, bot, 16, ty - 1).start()

    @pl.when(has_down)
    def _():
        halo(1, ROWS - 8, top, 0, ty + 1).start()

    for p in range(ntx - 1):
        @pl.when(p < tx)
        def _():
            pl.semaphore_signal(
                ready, inc=1, device_id={"ty": ty, "tx": p}, device_id_type=mesh_id
            )

    carries = lax.fori_loop(early, chunks // group, interior, carries)
    for k in range(VIEWS):
        msg_i[k] = carries[k][0:1]

    @pl.when(tx < ntx - 1)
    def _():
        pl.semaphore_wait(ready, ntx - 1 - tx)

    def message(msg, store, send, recv, p):
        return pltpu.make_async_remote_copy(
            src_ref=msg, dst_ref=store.at[tx], send_sem=send.at[p], recv_sem=recv.at[tx],
            device_id={"ty": ty, "tx": p}, device_id_type=mesh_id,
        )

    def spread(msg, store, send, recv):
        for p in range(1, ntx):
            @pl.when(p > tx)
            def _():
                message(msg, store, send, recv, p).start()

    def finish_sends(msg, store, send, recv):
        for p in range(1, ntx):
            @pl.when(p > tx)
            def _():
                message(msg, store, send, recv, p).wait_send()

    def receive(msg, store, recv):
        for p in range(ntx - 1):
            @pl.when(p < tx)
            def _():
                pltpu.make_async_remote_copy(
                    src_ref=msg, dst_ref=store.at[p], send_sem=recv.at[p], recv_sem=recv.at[p],
                    device_id={"ty": ty, "tx": p}, device_id_type=mesh_id,
                ).wait_recv()

    spread(msg_i, in_i, pre_send_i, pre_recv_i)

    @pl.when(has_down)
    def _():
        halo(0, 0, bot, 16, ty + 1).wait_recv()

    @pl.when(has_up)
    def _():
        halo(1, ROWS - 8, top, 0, ty - 1).wait_recv()

    edges = ((top, 0), (bot, ROWS - 8))
    bpeaks[...] = jnp.full(bpeaks.shape, NEG, jnp.float32)
    for k in range(VIEWS):
        for e, (src, row) in enumerate(edges):
            peak = None
            for c in range(chunks):
                part = lift(src, c, k, 8 + shift[k], ramp(k, c))
                ls[k, row:row + 8, c * LANES:(c + 1) * LANES] = part
                peak = part if peak is None else jnp.maximum(peak, part)
            bpeaks[16 * k + 8 * e:16 * k + 8 * e + 8, :] = peak
    msg_b[...] = jnp.max(bpeaks[...].T, axis=0, keepdims=True)
    spread(msg_b, in_b, pre_send_b, pre_recv_b)

    held[...] = jnp.full(held.shape, NEG, jnp.float32)

    def edge_scan(c, _):
        cols = pl.ds(pl.multiple_of(c * LANES, LANES), LANES)
        for k in range(VIEWS):
            for e, (_, row) in enumerate(edges):
                run = ls[k, row:row + 8, cols]
                step = 1
                while step < LANES:
                    run = jnp.maximum(
                        run, jnp.where(lane >= step, pltpu.roll(run, step, 1), NEG)
                    )
                    step *= 2
                run = jnp.maximum(run, held[2 * k + e])
                out[k, row:row + 8, cols] = run
                held[2 * k + e] = jnp.broadcast_to(run[:, LANES - 1:LANES], (8, LANES))
        return 0

    lax.fori_loop(0, chunks, edge_scan, 0)

    receive(msg_i, in_i, pre_recv_i)
    for k in range(VIEWS):
        best = in_i[0, k]
        for p in range(1, ntx):
            best = jnp.maximum(best, in_i[p, k])
        bsplat_i[k] = jnp.broadcast_to(best, (LANES, LANES)).T

    def close(k, row, before):
        for c in range(chunks):
            at = (k, pl.ds(row, 8), pl.ds(c * LANES, LANES))
            out[at] = jnp.maximum(out[at], before) - ls[at]

    def close_interior(i, _):
        row = pl.multiple_of(i * 8, 8)
        for k in range(VIEWS):
            close(k, row, bsplat_i[k, pl.ds(row, 8), :])
        return 0

    lax.fori_loop(1, tiles - 1, close_interior, 0)

    receive(msg_b, in_b, pre_recv_b)
    best = in_b[0]
    for p in range(1, ntx):
        best = jnp.maximum(best, in_b[p])
    bsplat_b[...] = jnp.broadcast_to(best, (LANES, LANES)).T
    for k in range(VIEWS):
        for e, (_, row) in enumerate(edges):
            close(k, row, bsplat_b[16 * k + 8 * e:16 * k + 8 * e + 8, :])

    @pl.when(has_up)
    def _():
        halo(0, 0, bot, 16, ty - 1).wait_send()

    @pl.when(has_down)
    def _():
        halo(1, ROWS - 8, top, 0, ty + 1).wait_send()

    finish_sends(msg_i, in_i, pre_send_i, pre_recv_i)
    finish_sends(msg_b, in_b, pre_send_b, pre_recv_b)


def on_device(surface_levels, bearing_index, stencil_displacements, camera_altitude_class):
    rows, width = surface_levels.shape
    nty, ntx = lax.axis_size("ty"), lax.axis_size("tx")
    chunks = width // LANES
    group, early = 2, 3
    vm = lambda *s: pltpu.VMEM(s, jnp.float32)
    arrays = [
        pltpu.with_memory_space_constraint(a, pltpu.HBM)
        for a in (surface_levels, bearing_index, stencil_displacements, camera_altitude_class)
    ]
    return pl.pallas_call(
        functools.partial(kernel, nty, ntx, chunks, group, early),
        out_shape=jax.ShapeDtypeStruct((VIEWS, rows, width), jnp.float32),
        in_specs=[pl.BlockSpec(memory_space=pltpu.HBM)] * 4,
        out_specs=pl.BlockSpec(memory_space=pltpu.VMEM),
        scratch_shapes=[
            pltpu.SMEM((VIEWS,), jnp.int32), pltpu.SMEM((VIEWS,), jnp.int32),
            pltpu.SMEM((VIEWS,), jnp.int32),
            vm(chunks, ROWS, LANES), vm(chunks, 24, LANES), vm(chunks, 24, LANES),
            vm(VIEWS, rows, width), vm(VIEWS, 5, 8, LANES),
            vm(group * VIEWS, 136, LANES), vm(group * VIEWS, 136, LANES),
            vm(LANES, LANES),
            vm(VIEWS, 1, LANES), vm(1, LANES),
            vm(ntx, VIEWS, 1, LANES), vm(ntx, 1, LANES),
            vm(VIEWS, LANES, LANES), vm(LANES, LANES), vm(2 * VIEWS, 8, LANES),
            pltpu.SemaphoreType.DMA((chunks,)),
            pltpu.SemaphoreType.DMA((3,)),
            pltpu.SemaphoreType.REGULAR,
            pltpu.SemaphoreType.DMA((2,)), pltpu.SemaphoreType.DMA((2,)),
            pltpu.SemaphoreType.DMA((ntx,)), pltpu.SemaphoreType.DMA((ntx,)),
            pltpu.SemaphoreType.DMA((ntx,)), pltpu.SemaphoreType.DMA((ntx,)),
        ],
        compiler_params=pltpu.CompilerParams(
            collective_id=0, has_side_effects=True, vmem_limit_bytes=40 * 1024 * 1024
        ),
        name="horizon",
    )(*arrays)


def solution(mesh):
    return jax.shard_map(
        on_device,
        mesh=mesh,
        in_specs=(P("ty", "tx"), P(), P(), P()),
        out_specs=P(None, "ty", "tx"),
        check_vma=False,
    )
```

time: 38.4 us -> 23 us (0.60)
  Pallas kernels: 33 us -> 20.8 us
  local copies, waits for them, and re-layouts: 5.2 us -> 2.02 us
    pallas_call x1, Pallas kernels: 33 us -> 20.8 us  [on_device(): pl.pallas_call(functools.partial(kernel, nty, ntx, chunks, group, early),...]
    unnamed x9 -> x1, local copies, waits for them, and re-layouts: 5.2 us -> 2.02 us
where the time goes in v2:
time: 23 us; the launch traced here: 22.8 us
  Pallas kernels  20.8 us (90%)
  local copies, waits for them, and re-layouts  2.02 us (9%)
    pallas_call x1, Pallas kernels, on_device(): pl.pallas_call(functools.partial(kernel, nty, ntx, chunks, group, early),...  20.8 us
    unnamed x1, local copies, waits for them, and re-layouts  2.02 us

profile of v2, /device:TPU:24, one launch (start us, length us, event | category | flops | bytes accessed | tf_op | source)
XLA Modules:
  0.0 22.8 jit_solution(9857570279281844429)
XLA Ops:
  0.0 20.8 %horizon.1 = f32[4,128,2048]{2,1,0:T(8,128)S(1)} custom-call(f32[128,2048]{1,0:T(8,128)} %x_hbm.1, s32[4]{0:T(128)} %bearing_hbm.1, s32[4]{0:T(128)} %shift_hbm.1, s32[4]{0:T(128)} %camera_hbm.1), custom_call_target="tpu_custom_call" | custom-call | tf_op jit(solution)/shard_map/horizon/pallas_call | solution.py:325
  20.8 2.0 %copy.6 = f32[4,128,2048]{2,1,0:T(8,128)} copy(f32[4,128,2048]{2,1,0:T(8,128)S(1)} %horizon.1) | data formatting | bytes 8388608

commit v3 on v2

v3 whole, which is shorter than its diff:
```python
import functools
import math

import jax
import jax.numpy as jnp
from jax import lax
from jax.experimental import pallas as pl
from jax.experimental.pallas import tpu as pltpu
from jax.sharding import PartitionSpec as P

VIEWS = 4
ROWS = 128
LANES = 128
NEG = -jnp.inf


def tables(bearing, camera, k, span):
    a = jnp.full((8, LANES), bearing[k], jnp.int32)
    cls = jnp.full((8, LANES), camera[k], jnp.int32).astype(jnp.float32)
    f = (((a * 5) & 15).astype(jnp.float32) + 0.5) / 16.0
    theta = (a.astype(jnp.float32) - 7.5) * (math.pi / 32.0)
    stride = 1.0 / jnp.cos(theta)
    slope = (1.0 + cls) / (4.0 * span)
    cube = f * f * f
    square = f * f
    taps = (
        (-cube + 2.0 * square - f) / 2.0,
        (3.0 * cube - 5.0 * square + 2.0) / 2.0,
        (-3.0 * cube + 4.0 * square + f) / 2.0,
        (cube - square) / 2.0,
    )
    return taps, stride * slope


def sub_scan(total, sub):
    for step in (1, 2, 4):
        total = jnp.maximum(total, jnp.where(sub >= step, pltpu.roll(total, step, 0), NEG))
    return total


def kernel(
    nty, ntx, chunks, group, lead, near, far,
    x_hbm, bearing_hbm, shift_hbm, camera_hbm, out,
    tab, xs, top, bot, ls, wv, slants, flat, scan,
    peaks, bpeaks, msg_i, msg_b, in_i, in_b, bsplat_i, bsplat_b,
    in_sem, top_sem, bot_sem, tab_sem, ready, halo_send, halo_recv,
    send_i, recv_i, send_b, recv_b,
):
    ty = lax.axis_index("ty")
    tx = lax.axis_index("tx")
    width = chunks * LANES
    span = width * ntx
    tiles = ROWS // 8
    half = chunks // 2
    has_up = ty > 0
    has_down = ty < nty - 1
    mesh_id = pl.DeviceIdType.MESH
    barrier = pltpu.get_barrier_semaphore()

    def greet(p):
        pl.semaphore_signal(barrier, inc=1, device_id=p, device_id_type=mesh_id)

    @pl.when(has_up)
    def _():
        greet({"ty": ty - 1, "tx": tx})

    @pl.when(has_down)
    def _():
        greet({"ty": ty + 1, "tx": tx})

    for p in range(1, ntx):
        @pl.when(p > tx)
        def _():
            greet({"ty": ty, "tx": p})

    for c in range(chunks):
        cols = pl.ds(c * LANES, LANES)
        pltpu.make_async_copy(
            x_hbm.at[pl.ds(0, 16), cols], top.at[c, pl.ds(8, 16)], top_sem
        ).start()
        pltpu.make_async_copy(
            x_hbm.at[pl.ds(ROWS - 16, 16), cols], bot.at[c, pl.ds(0, 16)], bot_sem
        ).start()
    small = [
        pltpu.make_async_copy(src, tab.at[n], tab_sem.at[n])
        for n, src in enumerate((bearing_hbm, shift_hbm, camera_hbm))
    ]
    for copy in small:
        copy.start()
    for c in range(chunks):
        pltpu.make_async_copy(
            x_hbm.at[:, pl.ds(c * LANES, LANES)], xs.at[c], in_sem
        ).start()

    in_i[...] = jnp.full(in_i.shape, NEG, jnp.float32)
    in_b[...] = jnp.full(in_b.shape, NEG, jnp.float32)
    blank = jnp.zeros((8, LANES), jnp.float32)
    lowest = jnp.full((8, LANES), NEG, jnp.float32)

    @pl.when(jnp.logical_not(has_up))
    def _():
        for c in range(chunks):
            top[c, 0:8] = blank

    @pl.when(jnp.logical_not(has_down))
    def _():
        for c in range(chunks):
            bot[c, 16:24] = blank

    def arrived(rows, cols, sem):
        pltpu.make_async_copy(
            x_hbm.at[pl.ds(0, rows), pl.ds(0, cols)],
            ls.at[0, pl.ds(0, rows), pl.ds(0, cols)], sem,
        ).wait()

    arrived(16, width, top_sem)
    arrived(16, width, bot_sem)

    pl.semaphore_wait(barrier, tx + has_up.astype(jnp.int32) + has_down.astype(jnp.int32))

    def halo(n, peer):
        if n == 0:
            src, dst = top.at[:, pl.ds(8, 6), :], bot.at[:, pl.ds(16, 6), :]
        else:
            src, dst = bot.at[:, pl.ds(11, 5), :], top.at[:, pl.ds(3, 5), :]
        return pltpu.make_async_remote_copy(
            src_ref=src, dst_ref=dst, send_sem=halo_send.at[n], recv_sem=halo_recv.at[n],
            device_id={"ty": peer, "tx": tx}, device_id_type=mesh_id,
        )

    @pl.when(has_up)
    def _():
        halo(0, ty - 1).start()

    @pl.when(has_down)
    def _():
        halo(1, ty + 1).start()

    for p in range(ntx - 1):
        @pl.when(p < tx)
        def _():
            pl.semaphore_signal(
                ready, inc=1, device_id={"ty": ty, "tx": p}, device_id_type=mesh_id
            )

    for copy in small:
        copy.wait()
    bearing, shift, camera = (
        [tab[n, k] for k in range(VIEWS)] for n in range(3)
    )
    lane = lax.broadcasted_iota(jnp.int32, (8, LANES), 1)
    sub = lax.broadcasted_iota(jnp.int32, (8, LANES), 0)
    first = tx * width
    for k in range(VIEWS):
        taps, rise = tables(bearing, camera, k, span)
        for j in range(4):
            wv[k, j] = taps[j]
        for c in range(chunks):
            slants[k, c] = rise * (lane + (first + c * LANES)).astype(jnp.float32)

    for k in range(VIEWS):
        peaks[k, 0:8, :] = lowest
        peaks[k, ROWS - 8:ROWS, :] = lowest

    arrived(ROWS, width, in_sem)

    def lift(src, c, k, start):
        acc = wv[k, 0] * src[c, pl.ds(start - 1, 8), :]
        for j in range(1, 4):
            acc = acc + wv[k, j] * src[c, pl.ds(start + j - 1, 8), :]
        return acc + slants[k, c]

    def lift_interior(i, _):
        row = pl.multiple_of(i * 8, 8)
        for k in range(VIEWS):
            peak = None
            for c in range(chunks):
                part = lift(xs, c, k, row + shift[k])
                ls[k, pl.ds(row, 8), c * LANES:(c + 1) * LANES] = part
                peak = part if peak is None else jnp.maximum(peak, part)
            peaks[k, pl.ds(row, 8), :] = peak
        return 0

    lax.fori_loop(1, tiles - 1, lift_interior, 0)
    for k in range(VIEWS):
        msg_i[k] = jnp.max(peaks[k].T, axis=0, keepdims=True)

    def spread(msg, store, send, recv):
        for p in range(ntx - 1, 0, -1):
            @pl.when(p > tx)
            def _():
                pltpu.make_async_remote_copy(
                    src_ref=msg, dst_ref=store.at[tx], send_sem=send, recv_sem=recv,
                    device_id={"ty": ty, "tx": p}, device_id_type=mesh_id,
                ).start()

    def all_of(store, send, recv, n):
        some = store.at[pl.ds(0, n)]
        return pltpu.make_async_remote_copy(
            src_ref=some, dst_ref=some, send_sem=send, recv_sem=recv,
            device_id={"ty": ty, "tx": tx}, device_id_type=mesh_id,
        )

    def finish_sends(store, send, recv):
        for n in range(1, ntx):
            @pl.when(ntx - 1 - tx == n)
            def _():
                all_of(store, send, recv, n).wait_send()

    def receive(store, send, recv):
        for n in range(1, ntx):
            @pl.when(tx == n)
            def _():
                all_of(store, send, recv, n).wait_recv()

    def turn_scan(parts, n, carry):
        turned = jnp.concatenate(parts, axis=0).T
        for t in range(16):
            at = 8 * t + t // 2
            flat[n, at:at + 8, :] = turned[8 * t:8 * t + 8]
        runs = [flat[n, pl.ds(0, 8, stride=17), :]]
        for u in range(1, 16):
            runs.append(jnp.maximum(runs[-1], flat[n, pl.ds(u, 8, stride=17), :]))
        total = sub_scan(runs[-1], sub)
        before = jnp.maximum(jnp.where(sub >= 1, pltpu.roll(total, 1, 0), NEG), carry)
        carry = jnp.maximum(carry, jnp.broadcast_to(total[7:8], (8, LANES)))
        for u in range(16):
            scan[n, pl.ds(u, 8, stride=17), :] = jnp.maximum(runs[u], before)
        whole = jnp.concatenate(
            [scan[n, 8 * t + t // 2:8 * t + t // 2 + 8, :] for t in range(16)], axis=0
        ).T
        return whole, carry

    def interior(g, carries):
        carries = list(carries)
        for q in range(group):
            c = g * group + q
            cols = pl.ds(pl.multiple_of(c * LANES, LANES), LANES)
            for k in range(VIEWS):
                parts = [blank] + [
                    ls[k, 8 * i:8 * i + 8, cols] for i in range(1, tiles - 1)
                ] + [blank]
                whole, carries[k] = turn_scan(parts, q * VIEWS + k, carries[k])
                for i in range(1, tiles - 1):
                    out[k, 8 * i:8 * i + 8, cols] = whole[8 * i:8 * i + 8]
        return tuple(carries)

    middle = jnp.logical_or(ty == nty // 2, ty == nty // 2 - 1)
    ahead = jnp.where(middle, far, near)
    carries = lax.fori_loop(0, lead, interior, (lowest,) * VIEWS)

    @pl.when(tx < ntx - 1)
    def _():
        pl.semaphore_wait(ready, ntx - 1 - tx)

    spread(msg_i, in_i, send_i, recv_i)
    carries = lax.fori_loop(lead, ahead, interior, carries)

    @pl.when(has_down)
    def _():
        halo(0, ty + 1).wait_recv()

    @pl.when(has_up)
    def _():
        halo(1, ty - 1).wait_recv()

    edges = ((top, 0), (bot, ROWS - 8))
    for k in range(VIEWS):
        for e, (src, row) in enumerate(edges):
            at = 16 * k + 8 * e
            halves = []
            for h in range(2):
                peak = None
                for c in range(h * half, (h + 1) * half):
                    part = lift(src, c, k, 8 + shift[k])
                    ls[k, row:row + 8, c * LANES:(c + 1) * LANES] = part
                    peak = part if peak is None else jnp.maximum(peak, part)
                halves.append(peak)
            bpeaks[at:at + 8, :] = jnp.maximum(halves[0], halves[1])
            bpeaks[64 + at:72 + at, :] = halves[0]
    msg_b[...] = jnp.max(bpeaks[...].T, axis=0, keepdims=True)
    spread(msg_b, in_b, send_b, recv_b)

    lax.fori_loop(ahead, chunks // group, interior, carries)

    carry = lowest
    for c in range(half):
        places = [
            (k, row, pl.ds((c + h * half) * LANES, LANES))
            for h in range(2) for k in range(VIEWS) for _, row in edges
        ]
        parts = [ls[k, row:row + 8, cols] for k, row, cols in places]
        whole, carry = turn_scan(parts, c, carry)
        for n, (k, row, cols) in enumerate(places):
            out[k, row:row + 8, cols] = whole[8 * n:8 * n + 8]

    receive(in_i, send_i, recv_i)
    for k in range(VIEWS):
        best = in_i[0, k]
        for p in range(1, ntx):
            best = jnp.maximum(best, in_i[p, k])
        bsplat_i[k] = jnp.broadcast_to(best, (LANES, LANES)).T

    def close(k, row, before, span):
        for c in span:
            at = (k, pl.ds(row, 8), pl.ds(c * LANES, LANES))
            out[at] = jnp.maximum(out[at], before) - ls[at]

    def close_interior(i, _):
        row = pl.multiple_of(i * 8, 8)
        for k in range(VIEWS):
            close(k, row, bsplat_i[k, pl.ds(row, 8), :], range(chunks))
        return 0

    lax.fori_loop(1, tiles - 1, close_interior, 0)

    @pl.when(has_up)
    def _():
        halo(0, ty - 1).wait_send()

    @pl.when(has_down)
    def _():
        halo(1, ty + 1).wait_send()

    finish_sends(in_i, send_i, recv_i)
    finish_sends(in_b, send_b, recv_b)

    receive(in_b, send_b, recv_b)
    best = in_b[0]
    for p in range(1, ntx):
        best = jnp.maximum(best, in_b[p])
    bsplat_b[...] = jnp.broadcast_to(best, (LANES, LANES)).T
    for k in range(VIEWS):
        for e, (_, row) in enumerate(edges):
            at = 16 * k + 8 * e
            before = bsplat_b[at:at + 8, :]
            close(k, row, before, range(half))
            own = jnp.max(bpeaks[64 + at:72 + at, :], axis=1, keepdims=True)
            close(k, row, jnp.maximum(before, own), range(half, chunks))


def on_device(surface_levels, bearing_index, stencil_displacements, camera_altitude_class):
    rows, width = surface_levels.shape
    nty, ntx = lax.axis_size("ty"), lax.axis_size("tx")
    chunks = width // LANES
    group, lead, near, far = 4, 0, 0, 1
    vm = lambda *s: pltpu.VMEM(s, jnp.float32)
    dma = pltpu.SemaphoreType.DMA
    arrays = [
        pltpu.with_memory_space_constraint(a, pltpu.HBM)
        for a in (surface_levels, bearing_index, stencil_displacements, camera_altitude_class)
    ]
    return pl.pallas_call(
        functools.partial(kernel, nty, ntx, chunks, group, lead, near, far),
        out_shape=jax.ShapeDtypeStruct((VIEWS, rows, width), jnp.float32),
        in_specs=[pl.BlockSpec(memory_space=pltpu.HBM)] * 4,
        out_specs=pl.BlockSpec(memory_space=pltpu.VMEM),
        scratch_shapes=[
            pltpu.SMEM((3, VIEWS), jnp.int32),
            vm(chunks, ROWS, LANES), vm(chunks, 24, LANES), vm(chunks, 24, LANES),
            vm(VIEWS, rows, width), vm(VIEWS, 4, 8, LANES), vm(VIEWS, chunks, 8, LANES),
            vm(group * VIEWS, 136, LANES), vm(group * VIEWS, 136, LANES),
            vm(VIEWS, ROWS, LANES), vm(LANES, LANES),
            vm(VIEWS, 1, LANES), vm(1, LANES),
            vm(ntx, VIEWS, 1, LANES), vm(ntx, 1, LANES),
            vm(VIEWS, LANES, LANES), vm(LANES, LANES),
            dma, dma, dma, dma((3,)),
            pltpu.SemaphoreType.REGULAR,
            dma((2,)), dma((2,)), dma, dma, dma, dma,
        ],
        compiler_params=pltpu.CompilerParams(
            collective_id=0, has_side_effects=True, vmem_limit_bytes=40 * 1024 * 1024
        ),
        name="horizon",
    )(*arrays)


def solution(mesh):
    return jax.shard_map(
        on_device,
        mesh=mesh,
        in_specs=(P("ty", "tx"), P(), P(), P()),
        out_specs=P(None, "ty", "tx"),
        check_vma=False,
    )
```

time: 23 us -> 16.2 us (0.70)
  Pallas kernels: 20.8 us -> 14 us
    pallas_call x1, Pallas kernels: 20.8 us -> 14 us  [on_device(): pl.pallas_call(functools.partial(kernel, nty, ntx, chunks, group, lead, n...]
where the time goes in v3:
time: 16.2 us; the launch traced here: 16 us
  Pallas kernels  14 us (86%)
  local copies, waits for them, and re-layouts  2.02 us (12%)
    pallas_call x1, Pallas kernels, on_device(): pl.pallas_call(functools.partial(kernel, nty, ntx, chunks, group, lead, n...  14 us
    unnamed x1, local copies, waits for them, and re-layouts  2.02 us

profile of v3, /device:TPU:24, one launch (start us, length us, event | category | flops | bytes accessed | tf_op | source)
XLA Modules:
  0.0 16.0 jit_solution(9690619058814861998)
XLA Ops:
  0.0 14.0 %horizon.1 = f32[4,128,2048]{2,1,0:T(8,128)S(1)} custom-call(f32[128,2048]{1,0:T(8,128)} %x_hbm.1, s32[4]{0:T(128)} %bearing_hbm.1, s32[4]{0:T(128)} %shift_hbm.1, s32[4]{0:T(128)} %camera_hbm.1), custom_call_target="tpu_custom_call" | custom-call | tf_op jit(solution)/shard_map/horizon/pallas_call | solution.py:353
  14.0 2.0 %copy.6 = f32[4,128,2048]{2,1,0:T(8,128)} copy(f32[4,128,2048]{2,1,0:T(8,128)S(1)} %horizon.1) | data formatting | bytes 8388608

commit v4 on v3

--- a/solution.py
+++ b/solution.py
@@ -39,11 +39,11 @@
 
 
 def kernel(
-    nty, ntx, chunks, group, lead, near, far,
+    nty, ntx, chunks, group, pre, near, far,
     x_hbm, bearing_hbm, shift_hbm, camera_hbm, out,
-    tab, xs, top, bot, ls, wv, slants, flat, scan,
+    tab, xs, top0, top1, bot0, bot1, ls, wv, slants, flat, scan,
     peaks, bpeaks, msg_i, msg_b, in_i, in_b, bsplat_i, bsplat_b,
-    in_sem, top_sem, bot_sem, tab_sem, ready, halo_send, halo_recv,
+    in_sem, top_sem, bot_sem, tab_sem, halo_send, halo_recv,
     send_i, recv_i, send_b, recv_b,
 ):
     ty = lax.axis_index("ty")
@@ -56,6 +56,7 @@
     has_down = ty < nty - 1
     mesh_id = pl.DeviceIdType.MESH
     barrier = pltpu.get_barrier_semaphore()
+    top, bot = (top0, top1), (bot0, bot1)
 
     def greet(p):
         pl.semaphore_signal(barrier, inc=1, device_id=p, device_id_type=mesh_id)
@@ -68,18 +69,19 @@
     def _():
         greet({"ty": ty + 1, "tx": tx})
 
-    for p in range(1, ntx):
-        @pl.when(p > tx)
+    for p in range(ntx - 1):
+        @pl.when(p < tx)
         def _():
             greet({"ty": ty, "tx": p})
 
     for c in range(chunks):
         cols = pl.ds(c * LANES, LANES)
         pltpu.make_async_copy(
-            x_hbm.at[pl.ds(0, 16), cols], top.at[c, pl.ds(8, 16)], top_sem
+            x_hbm.at[pl.ds(0, 16), cols], top[c // half].at[c % half, pl.ds(8, 16)], top_sem
         ).start()
         pltpu.make_async_copy(
-            x_hbm.at[pl.ds(ROWS - 16, 16), cols], bot.at[c, pl.ds(0, 16)], bot_sem
+            x_hbm.at[pl.ds(ROWS - 16, 16), cols], bot[c // half].at[c % half, pl.ds(0, 16)],
+            bot_sem,
         ).start()
     small = [
         pltpu.make_async_copy(src, tab.at[n], tab_sem.at[n])
@@ -92,20 +94,18 @@
             x_hbm.at[:, pl.ds(c * LANES, LANES)], xs.at[c], in_sem
         ).start()
 
-    in_i[...] = jnp.full(in_i.shape, NEG, jnp.float32)
-    in_b[...] = jnp.full(in_b.shape, NEG, jnp.float32)
     blank = jnp.zeros((8, LANES), jnp.float32)
     lowest = jnp.full((8, LANES), NEG, jnp.float32)
 
     @pl.when(jnp.logical_not(has_up))
     def _():
         for c in range(chunks):
-            top[c, 0:8] = blank
+            top[c // half][c % half, 0:8] = blank
 
     @pl.when(jnp.logical_not(has_down))
     def _():
         for c in range(chunks):
-            bot[c, 16:24] = blank
+            bot[c // half][c % half, 16:24] = blank
 
     def arrived(rows, cols, sem):
         pltpu.make_async_copy(
@@ -115,33 +115,6 @@
 
     arrived(16, width, top_sem)
     arrived(16, width, bot_sem)
-
-    pl.semaphore_wait(barrier, tx + has_up.astype(jnp.int32) + has_down.astype(jnp.int32))
-
-    def halo(n, peer):
-        if n == 0:
-            src, dst = top.at[:, pl.ds(8, 6), :], bot.at[:, pl.ds(16, 6), :]
-        else:
-            src, dst = bot.at[:, pl.ds(11, 5), :], top.at[:, pl.ds(3, 5), :]
-        return pltpu.make_async_remote_copy(
-            src_ref=src, dst_ref=dst, send_sem=halo_send.at[n], recv_sem=halo_recv.at[n],
-            device_id={"ty": peer, "tx": tx}, device_id_type=mesh_id,
-        )
-
-    @pl.when(has_up)
-    def _():
-        halo(0, ty - 1).start()
-
-    @pl.when(has_down)
-    def _():
-        halo(1, ty + 1).start()
-
-    for p in range(ntx - 1):
-        @pl.when(p < tx)
-        def _():
-            pl.semaphore_signal(
-                ready, inc=1, device_id={"ty": ty, "tx": p}, device_id_type=mesh_id
-            )
 
     for copy in small:
         copy.wait()
@@ -164,10 +137,10 @@
 
     arrived(ROWS, width, in_sem)
 
-    def lift(src, c, k, start):
-        acc = wv[k, 0] * src[c, pl.ds(start - 1, 8), :]
+    def lift(src, at, c, k, start):
+        acc = wv[k, 0] * src[at, pl.ds(start - 1, 8), :]
         for j in range(1, 4):
-            acc = acc + wv[k, j] * src[c, pl.ds(start + j - 1, 8), :]
+            acc = acc + wv[k, j] * src[at, pl.ds(start + j - 1, 8), :]
         return acc + slants[k, c]
 
     def lift_interior(i, _):
@@ -175,13 +148,40 @@
         for k in range(VIEWS):
             peak = None
             for c in range(chunks):
-                part = lift(xs, c, k, row + shift[k])
+                part = lift(xs, c, c, k, row + shift[k])
                 ls[k, pl.ds(row, 8), c * LANES:(c + 1) * LANES] = part
                 peak = part if peak is None else jnp.maximum(peak, part)
             peaks[k, pl.ds(row, 8), :] = peak
         return 0
 
-    lax.fori_loop(1, tiles - 1, lift_interior, 0)
+    lax.fori_loop(1, 1 + pre, lift_interior, 0)
+
+    pl.semaphore_wait(
+        barrier, (ntx - 1 - tx) + has_up.astype(jnp.int32) + has_down.astype(jnp.int32)
+    )
+
+    def halo(n, h, peer):
+        if n == 0:
+            src, dst = top[h].at[:, pl.ds(8, 6), :], bot[h].at[:, pl.ds(16, 6), :]
+        else:
+            src, dst = bot[h].at[:, pl.ds(11, 5), :], top[h].at[:, pl.ds(3, 5), :]
+        return pltpu.make_async_remote_copy(
+            src_ref=src, dst_ref=dst,
+            send_sem=halo_send.at[n, h], recv_sem=halo_recv.at[n, h],
+            device_id={"ty": peer, "tx": tx}, device_id_type=mesh_id,
+        )
+
+    @pl.when(has_up)
+    def _():
+        for h in range(2):
+            halo(0, h, ty - 1).start()
+
+    @pl.when(has_down)
+    def _():
+        for h in range(2):
+            halo(1, h, ty + 1).start()
+
+    lax.fori_loop(1 + pre, tiles - 1, lift_interior, 0)
     for k in range(VIEWS):
         msg_i[k] = jnp.max(peaks[k].T, axis=0, keepdims=True)
 
@@ -247,37 +247,29 @@
 
     middle = jnp.logical_or(ty == nty // 2, ty == nty // 2 - 1)
     ahead = jnp.where(middle, far, near)
-    carries = lax.fori_loop(0, lead, interior, (lowest,) * VIEWS)
-
-    @pl.when(tx < ntx - 1)
-    def _():
-        pl.semaphore_wait(ready, ntx - 1 - tx)
-
     spread(msg_i, in_i, send_i, recv_i)
-    carries = lax.fori_loop(lead, ahead, interior, carries)
-
-    @pl.when(has_down)
-    def _():
-        halo(0, ty + 1).wait_recv()
-
-    @pl.when(has_up)
-    def _():
-        halo(1, ty - 1).wait_recv()
+    carries = lax.fori_loop(0, ahead, interior, (lowest,) * VIEWS)
 
     edges = ((top, 0), (bot, ROWS - 8))
-    for k in range(VIEWS):
-        for e, (src, row) in enumerate(edges):
-            at = 16 * k + 8 * e
-            halves = []
-            for h in range(2):
-                peak = None
+    for h in range(2):
+        @pl.when(has_down)
+        def _():
+            halo(0, h, ty + 1).wait_recv()
+
+        @pl.when(has_up)
+        def _():
+            halo(1, h, ty - 1).wait_recv()
+
+        for k in range(VIEWS):
+            for e, (src, row) in enumerate(edges):
+                at = 16 * k + 8 * e
+                peak = None if h == 0 else bpeaks[64 + at:72 + at, :]
                 for c in range(h * half, (h + 1) * half):
-                    part = lift(src, c, k, 8 + shift[k])
+                    part = lift(src[h], c - h * half, c, k, 8 + shift[k])
                     ls[k, row:row + 8, c * LANES:(c + 1) * LANES] = part
                     peak = part if peak is None else jnp.maximum(peak, part)
-                halves.append(peak)
-            bpeaks[at:at + 8, :] = jnp.maximum(halves[0], halves[1])
-            bpeaks[64 + at:72 + at, :] = halves[0]
+                at = at + 64 if h == 0 else at
+                bpeaks[at:at + 8, :] = peak
     msg_b[...] = jnp.max(bpeaks[...].T, axis=0, keepdims=True)
     spread(msg_b, in_b, send_b, recv_b)
 
@@ -296,9 +288,9 @@
 
     receive(in_i, send_i, recv_i)
     for k in range(VIEWS):
-        best = in_i[0, k]
-        for p in range(1, ntx):
-            best = jnp.maximum(best, in_i[p, k])
+        best = jnp.full((1, LANES), NEG, jnp.float32)
+        for p in range(ntx - 1):
+            best = jnp.maximum(best, jnp.where(p < tx, in_i[p, k], NEG))
         bsplat_i[k] = jnp.broadcast_to(best, (LANES, LANES)).T
 
     def close(k, row, before, span):
@@ -316,19 +308,21 @@
 
     @pl.when(has_up)
     def _():
-        halo(0, ty - 1).wait_send()
+        for h in range(2):
+            halo(0, h, ty - 1).wait_send()
 
     @pl.when(has_down)
     def _():
-        halo(1, ty + 1).wait_send()
+        for h in range(2):
+            halo(1, h, ty + 1).wait_send()
 
     finish_sends(in_i, send_i, recv_i)
     finish_sends(in_b, send_b, recv_b)
 
     receive(in_b, send_b, recv_b)
-    best = in_b[0]
-    for p in range(1, ntx):
-        best = jnp.maximum(best, in_b[p])
+    best = jnp.full((1, LANES), NEG, jnp.float32)
+    for p in range(ntx - 1):
+        best = jnp.maximum(best, jnp.where(p < tx, in_b[p], NEG))
     bsplat_b[...] = jnp.broadcast_to(best, (LANES, LANES)).T
     for k in range(VIEWS):
         for e, (_, row) in enumerate(edges):
@@ -343,7 +337,7 @@
     rows, width = surface_levels.shape
     nty, ntx = lax.axis_size("ty"), lax.axis_size("tx")
     chunks = width // LANES
-    group, lead, near, far = 4, 0, 0, 1
+    group, pre, near, far = 4, 5, 1, 3
     vm = lambda *s: pltpu.VMEM(s, jnp.float32)
     dma = pltpu.SemaphoreType.DMA
     arrays = [
@@ -351,13 +345,13 @@
         for a in (surface_levels, bearing_index, stencil_displacements, camera_altitude_class)
     ]
     return pl.pallas_call(
-        functools.partial(kernel, nty, ntx, chunks, group, lead, near, far),
+        functools.partial(kernel, nty, ntx, chunks, group, pre, near, far),
         out_shape=jax.ShapeDtypeStruct((VIEWS, rows, width), jnp.float32),
         in_specs=[pl.BlockSpec(memory_space=pltpu.HBM)] * 4,
         out_specs=pl.BlockSpec(memory_space=pltpu.VMEM),
         scratch_shapes=[
             pltpu.SMEM((3, VIEWS), jnp.int32),
-            vm(chunks, ROWS, LANES), vm(chunks, 24, LANES), vm(chunks, 24, LANES),
+            vm(chunks, ROWS, LANES)] + [vm(chunks // 2, 24, LANES)] * 4 + [
             vm(VIEWS, rows, width), vm(VIEWS, 4, 8, LANES), vm(VIEWS, chunks, 8, LANES),
             vm(group * VIEWS, 136, LANES), vm(group * VIEWS, 136, LANES),
             vm(VIEWS, ROWS, LANES), vm(LANES, LANES),
@@ -365,8 +359,7 @@
             vm(ntx, VIEWS, 1, LANES), vm(ntx, 1, LANES),
             vm(VIEWS, LANES, LANES), vm(LANES, LANES),
             dma, dma, dma, dma((3,)),
-            pltpu.SemaphoreType.REGULAR,
-            dma((2,)), dma((2,)), dma, dma, dma, dma,
+            dma((2, 2)), dma((2, 2)), dma, dma, dma, dma,
         ],
         compiler_params=pltpu.CompilerParams(
             collective_id=0, has_side_effects=True, vmem_limit_bytes=40 * 1024 * 1024

time: 16.2 us -> 16.1 us (level)
  no operation moved by 1% of the time
where the time goes in v4:
time: 16.1 us; the launch traced here: 15.9 us
  Pallas kernels  13.9 us (86%)
  local copies, waits for them, and re-layouts  2.02 us (13%)
    pallas_call x1, Pallas kernels, on_device(): pl.pallas_call(functools.partial(kernel, nty, ntx, chunks, group, pre, ne...  13.9 us
    unnamed x1, local copies, waits for them, and re-layouts  2.02 us

profile of v4, /device:TPU:24, one launch (start us, length us, event | category | flops | bytes accessed | tf_op | source)
XLA Modules:
  0.0 15.9 jit_solution(5389426038134123002)
XLA Ops:
  0.0 13.9 %horizon.1 = f32[4,128,2048]{2,1,0:T(8,128)S(1)} custom-call(f32[128,2048]{1,0:T(8,128)} %x_hbm.1, s32[4]{0:T(128)} %bearing_hbm.1, s32[4]{0:T(128)} %shift_hbm.1, s32[4]{0:T(128)} %camera_hbm.1), custom_call_target="tpu_custom_call" | custom-call | tf_op jit(solution)/shard_map/horizon/pallas_call | solution.py:347
  13.9 2.0 %copy.6 = f32[4,128,2048]{2,1,0:T(8,128)} copy(f32[4,128,2048]{2,1,0:T(8,128)S(1)} %horizon.1) | data formatting | bytes 8388608

commit v5 on v4

--- a/solution.py
+++ b/solution.py
@@ -40,9 +40,9 @@
 
 def kernel(
     nty, ntx, chunks, group, pre, near, far,
-    x_hbm, bearing_hbm, shift_hbm, camera_hbm, out,
+    x_hbm, bearing_hbm, shift_hbm, camera_hbm, out, sums, before_b, firsts,
     tab, xs, top0, top1, bot0, bot1, ls, wv, slants, flat, scan,
-    peaks, bpeaks, msg_i, msg_b, in_i, in_b, bsplat_i, bsplat_b,
+    peaks, bpeaks, msg_i, msg_b, in_i, in_b, bsplat_i,
     in_sem, top_sem, bot_sem, tab_sem, halo_send, halo_recv,
     send_i, recv_i, send_b, recv_b,
 ):
@@ -186,7 +186,7 @@
         msg_i[k] = jnp.max(peaks[k].T, axis=0, keepdims=True)
 
     def spread(msg, store, send, recv):
-        for p in range(ntx - 1, 0, -1):
+        for p in list(range(ntx // 2, ntx)) + list(range(1, ntx // 2)):
             @pl.when(p > tx)
             def _():
                 pltpu.make_async_remote_copy(
@@ -266,8 +266,10 @@
                 peak = None if h == 0 else bpeaks[64 + at:72 + at, :]
                 for c in range(h * half, (h + 1) * half):
                     part = lift(src[h], c - h * half, c, k, 8 + shift[k])
-                    ls[k, row:row + 8, c * LANES:(c + 1) * LANES] = part
+                    sums[k, 8 * e:8 * e + 8, c * LANES:(c + 1) * LANES] = part
                     peak = part if peak is None else jnp.maximum(peak, part)
+                if h == 0:
+                    firsts[at:at + 8, :] = peak
                 at = at + 64 if h == 0 else at
                 bpeaks[at:at + 8, :] = peak
     msg_b[...] = jnp.max(bpeaks[...].T, axis=0, keepdims=True)
@@ -278,12 +280,13 @@
     carry = lowest
     for c in range(half):
         places = [
-            (k, row, pl.ds((c + h * half) * LANES, LANES))
-            for h in range(2) for k in range(VIEWS) for _, row in edges
+            (k, e, pl.ds((c + h * half) * LANES, LANES))
+            for h in range(2) for k in range(VIEWS) for e in range(2)
         ]
-        parts = [ls[k, row:row + 8, cols] for k, row, cols in places]
+        parts = [sums[k, 8 * e:8 * e + 8, cols] for k, e, cols in places]
         whole, carry = turn_scan(parts, c, carry)
-        for n, (k, row, cols) in enumerate(places):
+        for n, (k, e, cols) in enumerate(places):
+            row = edges[e][1]
             out[k, row:row + 8, cols] = whole[8 * n:8 * n + 8]
 
     receive(in_i, send_i, recv_i)
@@ -323,32 +326,60 @@
     best = jnp.full((1, LANES), NEG, jnp.float32)
     for p in range(ntx - 1):
         best = jnp.maximum(best, jnp.where(p < tx, in_b[p], NEG))
-    bsplat_b[...] = jnp.broadcast_to(best, (LANES, LANES)).T
+    before_b[...] = best
+
+
+def finish(x, sums, before_b, firsts, out, done, inner_sem, edge_sem):
+    half = x.shape[2] // LANES // 2
+    inner = pltpu.make_async_copy(
+        x.at[:, pl.ds(8, ROWS - 16)], out.at[:, pl.ds(8, ROWS - 16)], inner_sem
+    )
+    inner.start()
+    splat = jnp.broadcast_to(before_b[...], (LANES, LANES)).T
     for k in range(VIEWS):
-        for e, (_, row) in enumerate(edges):
+        for e, row in enumerate((0, ROWS - 8)):
             at = 16 * k + 8 * e
-            before = bsplat_b[at:at + 8, :]
-            close(k, row, before, range(half))
-            own = jnp.max(bpeaks[64 + at:72 + at, :], axis=1, keepdims=True)
-            close(k, row, jnp.maximum(before, own), range(half, chunks))
+            before = splat[at:at + 8, :]
+            own = jnp.max(firsts[at:at + 8, :], axis=1, keepdims=True)
+            for h, held in enumerate((before, jnp.maximum(before, own))):
+                for c in range(h * half, (h + 1) * half):
+                    cols = slice(c * LANES, (c + 1) * LANES)
+                    run = jnp.maximum(x[k, row:row + 8, cols], held)
+                    done[k, 8 * e:8 * e + 8, cols] = run - sums[k, 8 * e:8 * e + 8, cols]
+    copies = [
+        pltpu.make_async_copy(
+            done.at[:, pl.ds(8 * e, 8)], out.at[:, pl.ds(row, 8)], edge_sem.at[e]
+        )
+        for e, row in enumerate((0, ROWS - 8))
+    ]
+    for copy in copies:
+        copy.start()
+    for copy in copies:
+        copy.wait()
+    inner.wait()
 
 
 def on_device(surface_levels, bearing_index, stencil_displacements, camera_altitude_class):
     rows, width = surface_levels.shape
     nty, ntx = lax.axis_size("ty"), lax.axis_size("tx")
     chunks = width // LANES
-    group, pre, near, far = 4, 5, 1, 3
+    group, pre, near, far = 4, 5, 1, 2
     vm = lambda *s: pltpu.VMEM(s, jnp.float32)
     dma = pltpu.SemaphoreType.DMA
     arrays = [
         pltpu.with_memory_space_constraint(a, pltpu.HBM)
         for a in (surface_levels, bearing_index, stencil_displacements, camera_altitude_class)
     ]
-    return pl.pallas_call(
+    parts = pl.pallas_call(
         functools.partial(kernel, nty, ntx, chunks, group, pre, near, far),
-        out_shape=jax.ShapeDtypeStruct((VIEWS, rows, width), jnp.float32),
+        out_shape=[
+            jax.ShapeDtypeStruct(shape, jnp.float32)
+            for shape in (
+                (VIEWS, rows, width), (VIEWS, 16, width), (1, LANES), (LANES // 2, LANES)
+            )
+        ],
         in_specs=[pl.BlockSpec(memory_space=pltpu.HBM)] * 4,
-        out_specs=pl.BlockSpec(memory_space=pltpu.VMEM),
+        out_specs=[pl.BlockSpec(memory_space=pltpu.VMEM)] * 4,
         scratch_shapes=[
             pltpu.SMEM((3, VIEWS), jnp.int32),
             vm(chunks, ROWS, LANES)] + [vm(chunks // 2, 24, LANES)] * 4 + [
@@ -357,7 +388,7 @@
             vm(VIEWS, ROWS, LANES), vm(LANES, LANES),
             vm(VIEWS, 1, LANES), vm(1, LANES),
             vm(ntx, VIEWS, 1, LANES), vm(ntx, 1, LANES),
-            vm(VIEWS, LANES, LANES), vm(LANES, LANES),
+            vm(VIEWS, LANES, LANES),
             dma, dma, dma, dma((3,)),
             dma((2, 2)), dma((2, 2)), dma, dma, dma, dma,
         ],
@@ -366,6 +397,15 @@
         ),
         name="horizon",
     )(*arrays)
+    return pl.pallas_call(
+        finish,
+        out_shape=jax.ShapeDtypeStruct((VIEWS, rows, width), jnp.float32),
+        in_specs=[pl.BlockSpec(memory_space=pltpu.VMEM)] * 4,
+        out_specs=pl.BlockSpec(memory_space=pltpu.HBM),
+        scratch_shapes=[vm(VIEWS, 16, width), dma, dma((2,))],
+        compiler_params=pltpu.CompilerParams(vmem_limit_bytes=8 * 1024 * 1024),
+        name="finish",
+    )(*parts)
 
 
 def solution(mesh):

time: 16.1 us -> 15.9 us (0.988)
  local copies, waits for them, and re-layouts: 2.02 us -> 0 us
  Pallas kernels: 13.9 us -> 15.8 us
    pallas_call x0 -> x1, Pallas kernels: none -> 2.03 us  [on_device(): pl.pallas_call(finish, out_shape=jax.ShapeDtypeStruct((VIEWS, rows, width...]
    unnamed x1 -> x0, local copies, waits for them, and re-layouts: 2.02 us -> none
    pallas_call x1, Pallas kernels: 13.9 us -> 13.7 us  [on_device(): pl.pallas_call(functools.partial(kernel, nty, ntx, chunks, group, pre, ne...]
where the time goes in v5:
time: 15.9 us; the launch traced here: 15.8 us
  Pallas kernels  15.8 us (99%)
    pallas_call x1, Pallas kernels, on_device(): pl.pallas_call(functools.partial(kernel, nty, ntx, chunks, group, pre, ne...  13.7 us
    pallas_call x1, Pallas kernels, on_device(): pl.pallas_call(finish, out_shape=jax.ShapeDtypeStruct((VIEWS, rows, width...  2.03 us

profile of v5, /device:TPU:24, one launch (start us, length us, event | category | flops | bytes accessed | tf_op | source)
XLA Modules:
  0.0 15.8 jit_solution(622241743424865172)
XLA Ops:
  0.0 13.7 %horizon.1 = (f32[4,128,2048]{2,1,0:T(8,128)S(1)}, f32[4,16,2048]{2,1,0:T(8,128)S(1)}, f32[1,128]{1,0:T(1,128)S(1)}, f32[64,128]{1,0:T(8,128)S(1)}) custom-call(f32[128,2048]{1,0:T(8,128)} %x_hbm.1, s32[4]{0:T(128)} %bearing_hbm.1, s32[4]{0:T(128)} %shift_hbm.1, s32[4]{0:T(128)} %camera_hbm.1), custom_call_target="tpu_custom_call" | custom-call | tf_op jit(solution)/shard_map/horizon/pallas_call | solution.py:373
  13.7 2.0 %finish.1 = f32[4,128,2048]{2,1,0:T(8,128)} custom-call(f32[4,128,2048]{2,1,0:T(8,128)S(1)} %get-tuple-element.9.x, f32[4,16,2048]{2,1,0:T(8,128)S(1)} %get-tuple-element.10.sums, f32[1,128]{1,0:T(1,128)S(1)} %get-tuple-element.11.before_b, f32[64,128]{1,0:T(8,128)S(1)} %get-tuple-element.12.firsts), custom_call_target="tpu_custom_call" | custom-call | tf_op jit(solution)/shard_map/finish/pallas_call | solution.py:400

commit v6 on v5

--- a/solution.py
+++ b/solution.py
@@ -43,7 +43,7 @@
     x_hbm, bearing_hbm, shift_hbm, camera_hbm, out, sums, before_b, firsts,
     tab, xs, top0, top1, bot0, bot1, ls, wv, slants, flat, scan,
     peaks, bpeaks, msg_i, msg_b, in_i, in_b, bsplat_i,
-    in_sem, top_sem, bot_sem, tab_sem, halo_send, halo_recv,
+    in_sem, edge_in, tab_sem, halo_send, halo_recv,
     send_i, recv_i, send_b, recv_b,
 ):
     ty = lax.axis_index("ty")
@@ -77,11 +77,11 @@
     for c in range(chunks):
         cols = pl.ds(c * LANES, LANES)
         pltpu.make_async_copy(
-            x_hbm.at[pl.ds(0, 16), cols], top[c // half].at[c % half, pl.ds(8, 16)], top_sem
+            x_hbm.at[pl.ds(0, 16), cols], top[c // half].at[c % half, pl.ds(8, 16)], edge_in
         ).start()
         pltpu.make_async_copy(
             x_hbm.at[pl.ds(ROWS - 16, 16), cols], bot[c // half].at[c % half, pl.ds(0, 16)],
-            bot_sem,
+            edge_in,
         ).start()
     small = [
         pltpu.make_async_copy(src, tab.at[n], tab_sem.at[n])
@@ -113,8 +113,7 @@
             ls.at[0, pl.ds(0, rows), pl.ds(0, cols)], sem,
         ).wait()
 
-    arrived(16, width, top_sem)
-    arrived(16, width, bot_sem)
+    arrived(32, width, edge_in)
 
     for copy in small:
         copy.wait()
@@ -167,7 +166,7 @@
             src, dst = bot[h].at[:, pl.ds(11, 5), :], top[h].at[:, pl.ds(3, 5), :]
         return pltpu.make_async_remote_copy(
             src_ref=src, dst_ref=dst,
-            send_sem=halo_send.at[n, h], recv_sem=halo_recv.at[n, h],
+            send_sem=halo_send.at[n], recv_sem=halo_recv.at[n, h],
             device_id={"ty": peer, "tx": tx}, device_id_type=mesh_id,
         )
 
@@ -200,6 +199,13 @@
             src_ref=some, dst_ref=some, send_sem=send, recv_sem=recv,
             device_id={"ty": ty, "tx": tx}, device_id_type=mesh_id,
         )
+
+    def all_sent(n, count):
+        both = xs.at[:, pl.ds(0, count), :]
+        pltpu.make_async_remote_copy(
+            src_ref=both, dst_ref=both, send_sem=halo_send.at[n], recv_sem=halo_recv.at[n, 0],
+            device_id={"ty": ty, "tx": tx}, device_id_type=mesh_id,
+        ).wait_send()
 
     def finish_sends(store, send, recv):
         for n in range(1, ntx):
@@ -311,13 +317,11 @@
 
     @pl.when(has_up)
     def _():
-        for h in range(2):
-            halo(0, h, ty - 1).wait_send()
+        all_sent(0, 6)
 
     @pl.when(has_down)
     def _():
-        for h in range(2):
-            halo(1, h, ty + 1).wait_send()
+        all_sent(1, 5)
 
     finish_sends(in_i, send_i, recv_i)
     finish_sends(in_b, send_b, recv_b)
@@ -363,7 +367,7 @@
     rows, width = surface_levels.shape
     nty, ntx = lax.axis_size("ty"), lax.axis_size("tx")
     chunks = width // LANES
-    group, pre, near, far = 4, 5, 1, 2
+    group, pre, near, far = 4, 3, 1, 3
     vm = lambda *s: pltpu.VMEM(s, jnp.float32)
     dma = pltpu.SemaphoreType.DMA
     arrays = [
@@ -389,8 +393,8 @@
             vm(VIEWS, 1, LANES), vm(1, LANES),
             vm(ntx, VIEWS, 1, LANES), vm(ntx, 1, LANES),
             vm(VIEWS, LANES, LANES),
-            dma, dma, dma, dma((3,)),
-            dma((2, 2)), dma((2, 2)), dma, dma, dma, dma,
+            dma, dma, dma((3,)),
+            dma((2,)), dma((2, 2)), dma, dma, dma, dma,
         ],
         compiler_params=pltpu.CompilerParams(
             collective_id=0, has_side_effects=True, vmem_limit_bytes=40 * 1024 * 1024

time: 15.9 us -> 15.9 us (level)
  no operation moved by 1% of the time
where the time goes in v6:
time: 15.9 us; the launch traced here: 15.7 us
  Pallas kernels  15.7 us (99%)
    pallas_call x1, Pallas kernels, on_device(): pl.pallas_call(functools.partial(kernel, nty, ntx, chunks, group, pre, ne...  13.7 us
    pallas_call x1, Pallas kernels, on_device(): pl.pallas_call(finish, out_shape=jax.ShapeDtypeStruct((VIEWS, rows, width...  2.03 us

profile of v6, /device:TPU:24, one launch (start us, length us, event | category | flops | bytes accessed | tf_op | source)
XLA Modules:
  0.0 15.7 jit_solution(1603549791965756728)
XLA Ops:
  0.0 13.7 %horizon.1 = (f32[4,128,2048]{2,1,0:T(8,128)S(1)}, f32[4,16,2048]{2,1,0:T(8,128)S(1)}, f32[1,128]{1,0:T(1,128)S(1)}, f32[64,128]{1,0:T(8,128)S(1)}) custom-call(f32[128,2048]{1,0:T(8,128)} %x_hbm.1, s32[4]{0:T(128)} %bearing_hbm.1, s32[4]{0:T(128)} %shift_hbm.1, s32[4]{0:T(128)} %camera_hbm.1), custom_call_target="tpu_custom_call" | custom-call | tf_op jit(solution)/shard_map/horizon/pallas_call | solution.py:377
  13.7 2.0 %finish.1 = f32[4,128,2048]{2,1,0:T(8,128)} custom-call(f32[4,128,2048]{2,1,0:T(8,128)S(1)} %get-tuple-element.9.x, f32[4,16,2048]{2,1,0:T(8,128)S(1)} %get-tuple-element.10.sums, f32[1,128]{1,0:T(1,128)S(1)} %get-tuple-element.11.before_b, f32[64,128]{1,0:T(8,128)S(1)} %get-tuple-element.12.firsts), custom_call_target="tpu_custom_call" | custom-call | tf_op jit(solution)/shard_map/finish/pallas_call | solution.py:404

commit v7 on v6

--- a/solution.py
+++ b/solution.py
@@ -43,9 +43,11 @@
     x_hbm, bearing_hbm, shift_hbm, camera_hbm, out, sums, before_b, firsts,
     tab, xs, top0, top1, bot0, bot1, ls, wv, slants, flat, scan,
     peaks, bpeaks, msg_i, msg_b, in_i, in_b, bsplat_i,
-    in_sem, edge_in, tab_sem, halo_send, halo_recv,
-    send_i, recv_i, send_b, recv_b,
+    in_sem, edge_in, tab_sem, halo_recv,
+    recv_i, recv_b,
 ):
+    halo_send = (edge_in, in_sem)
+    send_i, send_b = tab_sem.at[0], tab_sem.at[1]
     ty = lax.axis_index("ty")
     tx = lax.axis_index("tx")
     width = chunks * LANES
@@ -166,7 +168,7 @@
             src, dst = bot[h].at[:, pl.ds(11, 5), :], top[h].at[:, pl.ds(3, 5), :]
         return pltpu.make_async_remote_copy(
             src_ref=src, dst_ref=dst,
-            send_sem=halo_send.at[n], recv_sem=halo_recv.at[n, h],
+            send_sem=halo_send[n], recv_sem=halo_recv.at[n, h],
             device_id={"ty": peer, "tx": tx}, device_id_type=mesh_id,
         )
 
@@ -203,7 +205,7 @@
     def all_sent(n, count):
         both = xs.at[:, pl.ds(0, count), :]
         pltpu.make_async_remote_copy(
-            src_ref=both, dst_ref=both, send_sem=halo_send.at[n], recv_sem=halo_recv.at[n, 0],
+            src_ref=both, dst_ref=both, send_sem=halo_send[n], recv_sem=halo_recv.at[n, 0],
             device_id={"ty": ty, "tx": tx}, device_id_type=mesh_id,
         ).wait_send()
 
@@ -394,7 +396,7 @@
             vm(ntx, VIEWS, 1, LANES), vm(ntx, 1, LANES),
             vm(VIEWS, LANES, LANES),
             dma, dma, dma((3,)),
-            dma((2,)), dma((2, 2)), dma, dma, dma, dma,
+            dma((2, 2)), dma, dma,
         ],
         compiler_params=pltpu.CompilerParams(
             collective_id=0, has_side_effects=True, vmem_limit_bytes=40 * 1024 * 1024

time: 15.9 us -> 15.9 us (level)
  no operation moved by 1% of the time
where the time goes in v7:
time: 15.9 us; the launch traced here: 15.7 us
  Pallas kernels  15.7 us (99%)
    pallas_call x1, Pallas kernels, on_device(): pl.pallas_call(functools.partial(kernel, nty, ntx, chunks, group, pre, ne...  13.7 us
    pallas_call x1, Pallas kernels, on_device(): pl.pallas_call(finish, out_shape=jax.ShapeDtypeStruct((VIEWS, rows, width...  2.03 us

profile of v7, /device:TPU:24, one launch (start us, length us, event | category | flops | bytes accessed | tf_op | source)
XLA Modules:
  0.0 15.7 jit_solution(18323707233055873103)
XLA Ops:
  0.0 13.7 %horizon.1 = (f32[4,128,2048]{2,1,0:T(8,128)S(1)}, f32[4,16,2048]{2,1,0:T(8,128)S(1)}, f32[1,128]{1,0:T(1,128)S(1)}, f32[64,128]{1,0:T(8,128)S(1)}) custom-call(f32[128,2048]{1,0:T(8,128)} %x_hbm.1, s32[4]{0:T(128)} %bearing_hbm.1, s32[4]{0:T(128)} %shift_hbm.1, s32[4]{0:T(128)} %camera_hbm.1), custom_call_target="tpu_custom_call" | custom-call | tf_op jit(solution)/shard_map/horizon/pallas_call | solution.py:379
  13.7 2.0 %finish.1 = f32[4,128,2048]{2,1,0:T(8,128)} custom-call(f32[4,128,2048]{2,1,0:T(8,128)S(1)} %get-tuple-element.9.x, f32[4,16,2048]{2,1,0:T(8,128)S(1)} %get-tuple-element.10.sums, f32[1,128]{1,0:T(1,128)S(1)} %get-tuple-element.11.before_b, f32[64,128]{1,0:T(8,128)S(1)} %get-tuple-element.12.firsts), custom_call_target="tpu_custom_call" | custom-call | tf_op jit(solution)/shard_map/finish/pallas_call | solution.py:406
